TPU v7x, 32 devices: a whole 2x2x4 slice. The times are simulated.
32 devices in a mesh: prob: 2 (over x), row: 4 (over z), col: 4 (over y, core).
Axes of the slice: x: 2, y: 2, z: 4, core: 2. Of those that a mesh axis runs over, the one named last changes fastest.
Arguments:
- kernel: bfloat16 [9216, 9216], P('row', 'col')
- cost_mat: bfloat16 [9216, 9216], P('row', 'col')
- src_mass: float32 [9216, 128], P('row', 'prob'), parts along dimension 1
- tgt_mass: float32 [9216, 128], P('col', 'prob'), parts along dimension 1
Outputs:
- output 1: float32 [9216, 128], P('row', 'prob'), parts along dimension 1
- output 2: float32 [9216, 128], P('col', 'prob'), parts along dimension 1
- output 3: float32 [128], P('prob'), parts along dimension 0
There are 2 independent parts. A program takes and returns all parts, laid end to end along the dimension named above; an argument that names none is the same for every part.
All inputs are finite; a program needn't handle non-finite values.
Results may differ from a plain program's by a relative error of at most 0.001.
Values are sent between devices in bfloat16 or wider.
A program may use at most 1 GiB of HBM per device.

v0:
```python
import jax
import jax.numpy as jnp
from jax import lax
from jax.sharding import PartitionSpec as P

SWEEPS = 6


def solution(mesh):
    row_size = mesh.shape["row"]
    col_size = mesh.shape["col"]

    def local_fn(kernel, cost_mat, src_mass, tgt_mass):
        tgt_scale = jnp.ones(tgt_mass.shape, jnp.float32)
        for sweep_idx in range(SWEEPS):
            row_part = jnp.dot(kernel, tgt_scale.astype(jnp.bfloat16), preferred_element_type=jnp.float32)
            src_scale = src_mass / lax.psum(row_part, "col")
            col_part = lax.dot_general(kernel, src_scale.astype(jnp.bfloat16), (((0,), (0,)), ((), ())), preferred_element_type=jnp.float32)
            tgt_scale = tgt_mass / lax.psum(col_part, "row")
        weighted = jnp.dot(kernel * cost_mat, tgt_scale.astype(jnp.bfloat16), preferred_element_type=jnp.float32)
        part_cost = jnp.sum(src_scale * weighted, axis=0)
        mass_norm = float(kernel.shape[0] * row_size * kernel.shape[1] * col_size)
        return src_scale, tgt_scale, lax.psum(part_cost, ("row", "col")) / mass_norm

    return jax.shard_map(local_fn, mesh=mesh, in_specs=(P("row", "col"), P("row", "col"), P("row", "prob"), P("col", "prob")), out_specs=(P("row", "prob"), P("col", "prob"), P("prob")), check_vma=False)
```

profile of v0, /device:TPU:0, one launch (start us, length us, event | category | flops | bytes accessed | tf_op | source)
XLA Modules:
  0.0 592.1 jit_solution(12389648307791311550)
XLA Ops:
  7.2 0.0 all-reduce.13.cloned.1.call-start
  7.2 8.2 %convolution_bitcast_fusion.11 = f32[2304,64]{0,1:T(8,128)} fusion(bf16[2304,2304]{1,0:T(8,128)(2,1)} %param.4), kind=kOutput, calls=%fused_computation.13 | convolution fusion | flops 679477248 | bytes 11206656 | tf_op jit(solution)/shard_map/dot_general | solution.py:16
  15.4 0.0 all-reduce.13.cloned.1.call-update
  15.5 0.0 all-reduce.15.cloned.1.call-start
  15.5 36.4 %all-reduce.13.cloned.1.call-done = f32[2304,64]{0,1:T(8,128)} async-done(((f32[2304,64]{0,1:T(8,128)}), f32[2304,64]{0,1:T(8,128)}) %all-reduce.13.cloned.1.call-update) | async-done | bytes 589840 | tf_op jit(solution)/shard_map/psum | solution.py:17
  51.9 7.0 %convolution_bitcast_fusion.10 = f32[2304,64]{0,1:T(8,128)} fusion(bf16[2304,2304]{1,0:T(8,128)(2,1)} %param.4, f32[2304,64]{0,1:T(8,128)S(1)} %copy-done, f32[2304,64]{0,1:T(8,128)} %all-reduce.13.cloned.1.call-done), kind=kOutput, calls=%fused_computation.12 | convolution fusion | flops 679772160 | bytes 12386304 | tf_op jit(solution)/shard_map/dot_general | solution.py:18
  58.8 0.0 all-reduce.15.cloned.1.call-update
  58.9 0.0 all-reduce.17.cloned.1.call-start
  58.9 40.1 %all-reduce.15.cloned.1.call-done = f32[2304,64]{0,1:T(8,128)} async-done(((f32[2304,64]{0,1:T(8,128)}), f32[2304,64]{0,1:T(8,128)}) %all-reduce.15.cloned.1.call-update) | async-done | bytes 589840 | tf_op jit(solution)/shard_map/psum | solution.py:19
  99.0 8.3 %convolution_bitcast_fusion.9 = f32[2304,64]{0,1:T(8,128)} fusion(bf16[2304,2304]{1,0:T(8,128)(2,1)} %param.4, f32[2304,64]{0,1:T(8,128)S(1)} %copy-done.1, f32[2304,64]{0,1:T(8,128)} %all-reduce.15.cloned.1.call-done), kind=kOutput, calls=%fused_computation.11 | convolution fusion | flops 679772160 | bytes 12386304 | tf_op jit(solution)/shard_map/dot_general | solution.py:16
  107.4 0.0 all-reduce.17.cloned.1.call-update
  107.4 0.0 all-reduce.19.cloned.1.call-start
  107.4 32.9 %all-reduce.17.cloned.1.call-done = f32[2304,64]{0,1:T(8,128)} async-done(((f32[2304,64]{0,1:T(8,128)}), f32[2304,64]{0,1:T(8,128)}) %all-reduce.17.cloned.1.call-update) | async-done | bytes 589840 | tf_op jit(solution)/shard_map/psum | solution.py:17
  140.3 7.0 %convolution_bitcast_fusion.8 = f32[2304,64]{0,1:T(8,128)} fusion(bf16[2304,2304]{1,0:T(8,128)(2,1)} %param.4, f32[2304,64]{0,1:T(8,128)S(1)} %copy-done, f32[2304,64]{0,1:T(8,128)} %all-reduce.17.cloned.1.call-done), kind=kOutput, calls=%fused_computation.10 | convolution fusion | flops 679772160 | bytes 12386304 | tf_op jit(solution)/shard_map/dot_general | solution.py:18
  147.3 0.0 all-reduce.19.cloned.1.call-update
  147.3 0.0 all-reduce.21.cloned.1.call-start
  147.4 40.0 %all-reduce.19.cloned.1.call-done = f32[2304,64]{0,1:T(8,128)} async-done(((f32[2304,64]{0,1:T(8,128)}), f32[2304,64]{0,1:T(8,128)}) %all-reduce.19.cloned.1.call-update) | async-done | bytes 589840 | tf_op jit(solution)/shard_map/psum | solution.py:19
  187.4 8.3 %convolution_bitcast_fusion.7 = f32[2304,64]{0,1:T(8,128)} fusion(bf16[2304,2304]{1,0:T(8,128)(2,1)} %param.4, f32[2304,64]{0,1:T(8,128)S(1)} %copy-done.1, f32[2304,64]{0,1:T(8,128)} %all-reduce.19.cloned.1.call-done), kind=kOutput, calls=%fused_computation.9 | convolution fusion | flops 679772160 | bytes 12386304 | tf_op jit(solution)/shard_map/dot_general | solution.py:16
  195.8 0.0 all-reduce.23.cloned.1.call-start
  195.9 32.9 %all-reduce.21.cloned.1.call-done = f32[2304,64]{0,1:T(8,128)} async-done(((f32[2304,64]{0,1:T(8,128)}), f32[2304,64]{0,1:T(8,128)}) %all-reduce.21.cloned.1.call-update) | async-done | bytes 589840 | tf_op jit(solution)/shard_map/psum | solution.py:17
  228.8 7.0 %convolution_bitcast_fusion.6 = f32[2304,64]{0,1:T(8,128)} fusion(bf16[2304,2304]{1,0:T(8,128)(2,1)} %param.4, f32[2304,64]{0,1:T(8,128)S(1)} %copy-done, f32[2304,64]{0,1:T(8,128)} %all-reduce.21.cloned.1.call-done), kind=kOutput, calls=%fused_computation.8 | convolution fusion | flops 679772160 | bytes 12386304 | tf_op jit(solution)/shard_map/dot_general | solution.py:18
  235.7 0.0 all-reduce.23.cloned.1.call-update
  235.8 0.0 all-reduce.25.cloned.1.call-start
  235.8 40.1 %all-reduce.23.cloned.1.call-done = f32[2304,64]{0,1:T(8,128)} async-done(((f32[2304,64]{0,1:T(8,128)}), f32[2304,64]{0,1:T(8,128)}) %all-reduce.23.cloned.1.call-update) | async-done | bytes 589840 | tf_op jit(solution)/shard_map/psum | solution.py:19
  275.9 8.3 %convolution_bitcast_fusion.5 = f32[2304,64]{0,1:T(8,128)} fusion(bf16[2304,2304]{1,0:T(8,128)(2,1)} %param.4, f32[2304,64]{0,1:T(8,128)S(1)} %copy-done.1, f32[2304,64]{0,1:T(8,128)} %all-reduce.23.cloned.1.call-done), kind=kOutput, calls=%fused_computation.7 | convolution fusion | flops 679772160 | bytes 12386304 | tf_op jit(solution)/shard_map/dot_general | solution.py:16
  284.2 0.0 all-reduce.25.cloned.1.call-update
  284.2 0.2 all-reduce.27.cloned.1.call-start
  284.5 32.7 %all-reduce.25.cloned.1.call-done = f32[2304,64]{0,1:T(8,128)} async-done(((f32[2304,64]{0,1:T(8,128)}), f32[2304,64]{0,1:T(8,128)}) %all-reduce.25.cloned.1.call-update) | async-done | bytes 589840 | tf_op jit(solution)/shard_map/psum | solution.py:17
  317.2 7.0 %convolution_bitcast_fusion.4 = f32[2304,64]{0,1:T(8,128)} fusion(bf16[2304,2304]{1,0:T(8,128)(2,1)} %param.4, f32[2304,64]{0,1:T(8,128)S(1)} %copy-done, f32[2304,64]{0,1:T(8,128)} %all-reduce.25.cloned.1.call-done), kind=kOutput, calls=%fused_computation.6 | convolution fusion | flops 679772160 | bytes 12386304 | tf_op jit(solution)/shard_map/dot_general | solution.py:18
  324.2 0.0 all-reduce.27.cloned.1.call-update
  324.2 0.0 all-reduce.29.cloned.1.call-start
  324.3 40.0 %all-reduce.27.cloned.1.call-done = f32[2304,64]{0,1:T(8,128)} async-done(((f32[2304,64]{0,1:T(8,128)}), f32[2304,64]{0,1:T(8,128)}) %all-reduce.27.cloned.1.call-update) | async-done | bytes 589840 | tf_op jit(solution)/shard_map/psum | solution.py:19
  364.3 8.3 %convolution_bitcast_fusion.3 = f32[2304,64]{0,1:T(8,128)} fusion(bf16[2304,2304]{1,0:T(8,128)(2,1)} %param.4, f32[2304,64]{0,1:T(8,128)S(1)} %copy-done.1, f32[2304,64]{0,1:T(8,128)} %all-reduce.27.cloned.1.call-done), kind=kOutput, calls=%fused_computation.5 | convolution fusion | flops 679772160 | bytes 12386304 | tf_op jit(solution)/shard_map/dot_general | solution.py:16
  372.7 0.0 all-reduce.31.cloned.1.call-start
  372.7 32.9 %all-reduce.29.cloned.1.call-done = f32[2304,64]{0,1:T(8,128)} async-done(((f32[2304,64]{0,1:T(8,128)}), f32[2304,64]{0,1:T(8,128)}) %all-reduce.29.cloned.1.call-update) | async-done | bytes 589840 | tf_op jit(solution)/shard_map/psum | solution.py:17
  405.6 7.0 %convolution_bitcast_fusion.2 = f32[2304,64]{0,1:T(8,128)} fusion(bf16[2304,2304]{1,0:T(8,128)(2,1)} %param.4, f32[2304,64]{0,1:T(8,128)S(1)} %copy-done, f32[2304,64]{0,1:T(8,128)} %all-reduce.29.cloned.1.call-done), kind=kOutput, calls=%fused_computation.4 | convolution fusion | flops 679772160 | bytes 12386304 | tf_op jit(solution)/shard_map/dot_general | solution.py:18
  412.6 0.0 all-reduce.33.cloned.1.call-start
  412.7 40.1 %all-reduce.31.cloned.1.call-done = f32[2304,64]{0,1:T(8,128)} async-done(((f32[2304,64]{0,1:T(8,128)}), f32[2304,64]{0,1:T(8,128)}) %all-reduce.31.cloned.1.call-update) | async-done | bytes 589840 | tf_op jit(solution)/shard_map/psum | solution.py:19
  452.7 8.3 %convolution_bitcast_fusion.1 = f32[2304,64]{0,1:T(8,128)} fusion(bf16[2304,2304]{1,0:T(8,128)(2,1)} %param.4, f32[2304,64]{0,1:T(8,128)S(1)} %copy-done.1, f32[2304,64]{0,1:T(8,128)} %all-reduce.31.cloned.1.call-done), kind=kOutput, calls=%fused_computation.3 | convolution fusion | flops 679772160 | bytes 12386304 | tf_op jit(solution)/shard_map/dot_general | solution.py:16
  461.1 0.0 all-reduce.35.cloned.1.call-start
  461.2 32.9 %all-reduce.33.cloned.1.call-done = f32[2304,64]{0,1:T(8,128)} async-done(((f32[2304,64]{0,1:T(8,128)}), f32[2304,64]{0,1:T(8,128)}) %all-reduce.33.cloned.1.call-update) | async-done | bytes 589840 | tf_op jit(solution)/shard_map/psum | solution.py:17
  494.1 1.1 div.52
  495.2 7.0 %convolution_bitcast_fusion = f32[2304,64]{0,1:T(8,128)} fusion(bf16[2304,2304]{1,0:T(8,128)(2,1)} %param.4, f32[2304,64]{0,1:T(8,128)S(1)} %div.52), kind=kOutput, calls=%fused_computation.2 | convolution fusion | flops 679624704 | bytes 11796480 | tf_op jit(solution)/shard_map/dot_general | solution.py:18
  502.2 40.1 %all-reduce.35.cloned.1.call-done = f32[2304,64]{0,1:T(8,128)} async-done(((f32[2304,64]{0,1:T(8,128)}), f32[2304,64]{0,1:T(8,128)}) %all-reduce.35.cloned.1.call-update) | async-done | bytes 589840 | tf_op jit(solution)/shard_map/psum | solution.py:19
  542.3 1.1 div.53
  543.5 10.7 %fusion.5 = f32[64]{0:T(128)S(1)} fusion(f32[2304,64]{0,1:T(8,128)S(1)} %div.52, bf16[2304,2304]{1,0:T(8,128)(2,1)} %param.4, bf16[2304,2304]{1,0:T(8,128)(2,1)} %param.5, f32[2304,64]{0,1:T(8,128)S(1)} %div.53), kind=kOutput, calls=%fused_computation.15 | convolution fusion | flops 685227968 | bytes 22413568 | tf_op jit(solution)/shard_map/dot_general | solution.py:20
  554.2 30.5 %psum.103 = f32[64]{0:T(128)S(1)} all-reduce(f32[64]{0:T(128)S(1)} %fusion.5), channel_id=1, replica_groups=mesh['prob'=2,'row'=4,'col'=4] {'row','col'}, use_global_device_ids=true, to_apply=%region_13.0 | all-reduce | flops 64 | bytes 512 | tf_op jit(solution)/shard_map/psum | solution.py:23
  584.7 0.5 broadcast_multiply_fusion
  (13 shorter events, 0.1 us)
Async XLA Ops:
  7.2 44.7 %copy-start = (f32[2304,64]{0,1:T(8,128)S(1)}, f32[2304,64]{0,1:T(8,128)}, u32[]{:S(2)}) copy-start(f32[2304,64]{0,1:T(8,128)} %param.6) | copy-start | bytes 1769476
  7.2 44.7 %all-reduce.13.cloned.1.call-start = ((), (), s32[]{:S(2)}) async-start(), calls=%async_computation | async-start | bytes 1179648 | tf_op jit(solution)/shard_map/psum | solution.py:17
  15.4 83.6 %copy-start.1 = (f32[2304,64]{0,1:T(8,128)S(1)}, f32[2304,64]{0,1:T(8,128)}, u32[]{:S(2)}) copy-start(f32[2304,64]{0,1:T(8,128)} %param.7) | copy-start | bytes 1769476
  15.5 83.6 %all-reduce.15.cloned.1.call-start = ((), (), s32[]{:S(2)}) async-start(), calls=%async_computation.1 | async-start | bytes 1179648 | tf_op jit(solution)/shard_map/psum | solution.py:19
  58.9 81.5 %all-reduce.17.cloned.1.call-start = ((), (), s32[]{:S(2)}) async-start(), calls=%async_computation.2 | async-start | bytes 1179648 | tf_op jit(solution)/shard_map/psum | solution.py:17
  107.4 80.0 %all-reduce.19.cloned.1.call-start = ((), (), s32[]{:S(2)}) async-start(), calls=%async_computation.3 | async-start | bytes 1179648 | tf_op jit(solution)/shard_map/psum | solution.py:19
  147.3 81.4 %all-reduce.21.cloned.1.call-start = ((), (), s32[]{:S(2)}) async-start(), calls=%async_computation.4 | async-start | bytes 1179648 | tf_op jit(solution)/shard_map/psum | solution.py:17
  195.8 80.1 %all-reduce.23.cloned.1.call-start = ((), (), s32[]{:S(2)}) async-start(), calls=%async_computation.5 | async-start | bytes 1179648 | tf_op jit(solution)/shard_map/psum | solution.py:19
  235.8 81.4 %all-reduce.25.cloned.1.call-start = ((), (), s32[]{:S(2)}) async-start(), calls=%async_computation.6 | async-start | bytes 1179648 | tf_op jit(solution)/shard_map/psum | solution.py:17
  284.2 80.0 %all-reduce.27.cloned.1.call-start = ((), (), s32[]{:S(2)}) async-start(), calls=%async_computation.7 | async-start | bytes 1179648 | tf_op jit(solution)/shard_map/psum | solution.py:19
  324.2 81.4 %all-reduce.29.cloned.1.call-start = ((), (), s32[]{:S(2)}) async-start(), calls=%async_computation.8 | async-start | bytes 1179648 | tf_op jit(solution)/shard_map/psum | solution.py:17
  372.7 80.1 %all-reduce.31.cloned.1.call-start = ((), (), s32[]{:S(2)}) async-start(), calls=%async_computation.9 | async-start | bytes 1179648 | tf_op jit(solution)/shard_map/psum | solution.py:19
  412.6 81.4 %all-reduce.33.cloned.1.call-start = ((), (), s32[]{:S(2)}) async-start(), calls=%async_computation.10 | async-start | bytes 1179648 | tf_op jit(solution)/shard_map/psum | solution.py:17
  461.1 81.2 %all-reduce.35.cloned.1.call-start = ((), (), s32[]{:S(2)}) async-start(), calls=%async_computation.11 | async-start | bytes 1179648 | tf_op jit(solution)/shard_map/psum | solution.py:19
  495.2 48.2 %copy-start.2 = (f32[2304,64]{0,1:T(8,128)}, f32[2304,64]{0,1:T(8,128)S(1)}, u32[]{:S(2)}) copy-start(f32[2304,64]{0,1:T(8,128)S(1)} %div.52) | copy-start | bytes 1769476
  543.5 10.7 %copy-start.3 = (f32[2304,64]{0,1:T(8,128)}, f32[2304,64]{0,1:T(8,128)S(1)}, u32[]{:S(2)}) copy-start(f32[2304,64]{0,1:T(8,128)S(1)} %div.53) | copy-start | bytes 1769476
Sparse Core Ops, SparseCore 0:
  15.6 36.2 all-reduce.12
  59.0 39.9 all-reduce.14
  107.5 32.7 all-reduce.16
  147.5 39.9 all-reduce.18
  195.9 32.7 all-reduce.20
  235.9 39.9 all-reduce.22
  284.4 32.7 all-reduce.24
  324.3 39.9 all-reduce.26
  372.8 32.7 all-reduce.28
  412.8 39.9 all-reduce.30
  461.2 32.7 all-reduce.32
  502.4 39.9 all-reduce.34
where the time goes:
time: 593 us; the launch traced here: 592 us
  waiting for transfers between devices  441 us (74%)
  matrix products  102 us (17%)
  blocking collectives  30.5 us (5%)
  between operations  14.3 us (2%)
    psum x6, waiting for transfers between devices, local_fn(): tgt_scale = tgt_mass / lax.psum(col_part, 'row')  240 us
    psum x6, waiting for transfers between devices, local_fn(): src_scale = src_mass / lax.psum(row_part, 'col')  201 us
    dot_general x6, matrix products, local_fn(): jnp.dot(kernel, tgt_scale.astype(jnp.bfloat16), preferred_element_type=jn...  49.9 us
    dot_general x6, matrix products, local_fn(): lax.dot_general(kernel, src_scale.astype(jnp.bfloat16), (((0,), (0,)), ((...  41.9 us
    psum x1, blocking collectives, local_fn(): lax.psum(part_cost, ('row', 'col')) / mass_norm  30.5 us
  transfers between devices with their start and end apart: 12, of which 12 were waited for; matrix products, arithmetic and copies ran while one was open for 0% of the time, Pallas kernels for 0%

commit v1 on v0

v1 whole, which is shorter than its diff:
```python
import functools

import jax
import jax.numpy as jnp
from jax import lax
from jax.experimental import pallas as pl
from jax.experimental.pallas import tpu as pltpu
from jax.sharding import PartitionSpec as P

SWEEPS = 6
MESH = pl.DeviceIdType.MESH
F32 = jnp.float32
BF16 = jnp.bfloat16
NB = 2
NT = 3


def dot_nn(x, y):
    return jnp.dot(x, y, preferred_element_type=F32)


def dot_nt(x, y):
    return lax.dot_general(x, y, (((1,), (1,)), ((), ())), preferred_element_type=F32)


def tiles(size, tile=256):
    return [(o, min(tile, size - o)) for o in range(0, size, tile)]


def kernel(n_row, n_col, norm,
           k_hbm, c_hbm, a_hbm, b_hbm, u_hbm, v_hbm, cost_ref,
           K, C, A, B, UB, VB, UF, VF, DS, DR, SP, YR, TP, EI, XR, R0, ACC, CPS, CPR,
           k_sem, in_sem, out_sem, r0_sem,
           d_sem, y_sem, u_sem, uf_sem, e_sem, x_sem, v_sem, vf_sem, cp_sem):
    row = lax.axis_index("row")
    col = lax.axis_index("col")
    core = lax.rem(col, 2)
    n = K.shape[0]
    half = n // 2
    m = UB.shape[1]
    width = n // NT
    sib = {"col": col + 1 - 2 * core}
    ypeer = {"col": lax.rem(col + 2, n_col)}
    inner = jnp.logical_or(row == 1, row == 2)
    edge = jnp.logical_not(inner)
    zpair = {"row": row + 1 - 2 * lax.rem(row, 2)}
    zmid = {"row": n_row - 1 - row}
    own0 = pl.multiple_of(core * half, 128)
    sib0 = pl.multiple_of((1 - core) * half, 128)
    subs = [(0, 512), (512, half - 512)]

    def rcopy(src, dst, sem, dev):
        return pltpu.make_async_remote_copy(src_ref=src, dst_ref=dst, send_sem=sem.at[0], recv_sem=sem.at[1],
                                            device_id=dev, device_id_type=MESH)

    rows_per = 384
    k_loads = []
    for h0 in (sib0, own0):
        for j in range(half // rows_per):
            sl = pl.ds(pl.multiple_of(h0 + j * rows_per, 128), rows_per)
            cp = pltpu.make_async_copy(k_hbm.at[sl, :], K.at[sl, :], k_sem.at[len(k_loads)])
            cp.start()
            k_loads.append((sl, cp))
    a_load = pltpu.make_async_copy(a_hbm, A, in_sem.at[0])
    b_load = pltpu.make_async_copy(b_hbm, B, in_sem.at[1])
    c_load = pltpu.make_async_copy(c_hbm, C, in_sem.at[2])
    a_load.start()
    b_load.start()
    c_load.start()

    barrier = pltpu.get_barrier_semaphore()
    rel = [(dr, dc) for dr in range(n_row) for dc in range(n_col) if (dr, dc) != (0, 0)]
    peers = [{"row": lax.rem(row + dr, n_row), "col": lax.rem(col + dc, n_col)} for dr, dc in rel]
    for dev in peers:
        pl.semaphore_signal(barrier, inc=1, device_id=dev, device_id_type=MESH)

    ACC[...] = jnp.zeros_like(ACC)

    ones = jnp.ones((16, n), BF16)
    per_half = half // rows_per
    for h in range(2):
        for j in range(per_half):
            sl, cp = k_loads[h * per_half + j]
            cp.wait()
            R0[h, :, j * rows_per:(j + 1) * rows_per] = dot_nt(ones, K[sl, :])[:8]
        if h == 0:
            pl.semaphore_wait(barrier, len(peers))
            r0d = rcopy(R0.at[0], R0.at[2], r0_sem.at[0], sib)
            r0d.start()
    r0d.wait()
    R0[1] = R0[1] + R0[2]
    r0y = rcopy(R0.at[1], R0.at[3], r0_sem.at[1], ypeer)
    r0y.start()
    a_load.wait()
    r0y.wait()
    s0 = R0[1, 0:1] + R0[3, 0:1]

    def u_copy(b, j):
        o, w = subs[j]
        ref = UB.at[b, :, pl.ds(pl.multiple_of(own0 + o, 128), w)]
        return rcopy(ref, ref, u_sem.at[b, j], sib)

    def uf_copy(b):
        ref = UF.at[b, :, pl.ds(own0, half)]
        return rcopy(ref, ref, uf_sem.at[b], sib)

    for b in range(NB):
        for j, (o, w) in enumerate(subs):
            sl = pl.ds(pl.multiple_of(own0 + o, 128), w)
            UB[b, :, sl] = (A[pl.ds(b * m, m), sl] / s0[:, o:o + w]).astype(BF16)
            u_copy(b, j).start()
    b_load.wait()

    def when(cond, fn):
        pl.when(cond)(fn)

    def s_steps(b, sweep):
        par = lax.rem(sweep, 2)
        last = sweep == SWEEPS - 1

        def d_copy():
            return rcopy(DS.at[b], DR.at[b], d_sem.at[b], sib)

        def y_copy(j):
            o, w = subs[j]
            return rcopy(SP.at[b, :, pl.ds(o, w)], YR.at[par, b, :, pl.ds(o, w)], y_sem.at[par, b, j], ypeer)

        def s1():
            for o, w in tiles(half):
                DS[b, :, o:o + w] = dot_nt(VB[b], K[pl.ds(pl.multiple_of(sib0 + o, 128), w), :])
            d_copy().start()

        def s2():
            for o, w in tiles(half):
                SP[b, :, o:o + w] = dot_nt(VB[b], K[pl.ds(pl.multiple_of(own0 + o, 128), w), :])

        def s3():
            d_copy().wait_recv()
            for j, (o, w) in enumerate(subs):
                SP[b, :, o:o + w] = SP[b, :, o:o + w] + DR[b, :, o:o + w]
                y_copy(j).start()

        def s4(j):
            def run():
                o, w = subs[j]
                y_copy(j).wait_recv()
                sl = pl.ds(pl.multiple_of(own0 + o, 128), w)
                u = A[pl.ds(b * m, m), sl] / (SP[b, :, o:o + w] + YR[par, b, :, o:o + w])
                UB[b, :, sl] = u.astype(BF16)
                u_copy(b, j).start()
                UF[b, :, sl] = u
                if j == len(subs) - 1:
                    when(last, lambda: uf_copy(b).start())
                    d_copy().wait_send()
                y_copy(j).wait_send()
            return run

        return {"s1": s1, "s2": s2, "s3": s3, "s40": s4(0), "s41": s4(1)}

    def t_steps(b, sweep, last):
        par = lax.rem(sweep, 2)

        def piece(c):
            return pl.ds(c * width, width)

        def e_copy(c):
            return rcopy(TP.at[b, :, piece(c)], EI.at[b, :, piece(c)], e_sem.at[b, c], zpair)

        def x_copy(c):
            return rcopy(TP.at[b, :, piece(c)], XR.at[par, b, :, piece(c)], x_sem.at[par, b, c], zmid)

        def v_copy(c):
            ref = VB.at[b, :, piece(c)]
            return rcopy(ref, ref, v_sem.at[b, c], zpair)

        def vf_copy(c):
            ref = VF.at[b, :, piece(c)]
            return rcopy(ref, ref, vf_sem.at[b, c], zpair)

        def t0():
            for j in range(len(subs)):
                u_copy(b, j).wait()

        def t1(c):
            def run():
                for o, w in tiles(width):
                    o += c * width
                    TP[b, :, o:o + w] = dot_nn(UB[b], K[:, o:o + w])
                when(edge, lambda: e_copy(c).start())
            return run

        def t2(c):
            def at_inner():
                e_copy(c).wait_recv()
                TP[b, :, piece(c)] = TP[b, :, piece(c)] + EI[b, :, piece(c)]
                x_copy(c).start()
            return lambda: when(inner, at_inner)

        def t3(c):
            def at_inner():
                x_copy(c).wait_recv()
                v = B[pl.ds(b * m, m), piece(c)] / (TP[b, :, piece(c)] + XR[par, b, :, piece(c)])
                VB[b, :, piece(c)] = v.astype(BF16)
                v_copy(c).start()
                VF[b, :, piece(c)] = v
                when(last, lambda: vf_copy(c).start())
                x_copy(c).wait_send()
                v_copy(c).wait_send()

            def at_edge():
                v_copy(c).wait_recv()
                e_copy(c).wait_send()

            def run():
                when(inner, at_inner)
                when(edge, at_edge)
            return run

        def fin():
            for c in range(NT):
                when(inner, lambda: vf_copy(c).wait_send())
                when(edge, lambda: vf_copy(c).wait_recv())

        steps = {"t0": t0, "fin": fin}
        for c in range(NT):
            steps["t1%d" % c] = t1(c)
            steps["t2%d" % c] = t2(c)
            steps["t3%d" % c] = t3(c)
        return steps

    def kc_rows(i, rows):
        sl = pl.ds(pl.multiple_of(i * rows, rows), rows)
        C[sl, :] = K[sl, :] * C[sl, :]

    def cost_step(b):
        acc = jnp.zeros((m, 128), F32)
        for o, w in tiles(n):
            p = UF[b, :, o:o + w] * dot_nt(VB[b], C[o:o + w, :])
            for q in range(0, w, 128):
                acc = acc + p[:, q:q + 128]
        ACC[b * m:(b + 1) * m, :] = acc

    def run(steps, *names):
        for group in names:
            for name in group.split():
                steps[name]()

    def named(prefix, *dicts):
        return {prefix + k: f for d in dicts for k, f in d.items()}

    no = jnp.bool_(False)
    yes = jnp.bool_(True)
    st = {**named("A", t_steps(0, 0, no)), **named("B", t_steps(1, 0, no))}
    run(st, "At0 At10 At11 At12")
    c_load.wait()
    run(st, "At20 At21 At22", "At30", "Bt0 Bt10 Bt11 Bt12", "At31 At32")

    def body(s, carry):
        last = s + 1 == SWEEPS - 1
        st = {**named("A", s_steps(0, s + 1), t_steps(0, s + 1, last)), **named("B", s_steps(1, s + 1))}
        old = named("b", t_steps(1, s, no))
        new = named("B", t_steps(1, s + 1, no))
        st = {**new, **st, **old, "kc": lambda: kc_rows(s, 384)}
        run(st, "As1 As2 bt20 As3", "kc bt21 bt22", "As40 bt30 As41 bt31", "At0 At10 At11 At12", "bt32",
            "Bs1 Bs2 At20 Bs3", "At21 At22", "Bs40 At30 Bs41 At31", "Bt0 Bt10 Bt11 Bt12", "At32")
        return carry

    lax.fori_loop(0, SWEEPS - 1, body, 0)

    kc_rows(SWEEPS - 1, 384)
    stb = named("B", t_steps(1, SWEEPS - 1, yes))
    sta = named("A", t_steps(0, SWEEPS - 1, yes))
    uf_copy(0).wait()
    run(stb, "Bt20 Bt21 Bt22")
    cost_step(0)
    run(stb, "Bt30 Bt31 Bt32")
    uf_copy(1).wait()
    u_out = [pltpu.make_async_copy(UF.at[b], u_hbm.at[pl.ds(b * m, m), :], out_sem.at[b]) for b in range(NB)]
    for cp in u_out:
        cp.start()
    cost_step(1)
    tot = jnp.sum(jnp.transpose(ACC[...]), axis=0, keepdims=True)
    CPS[...] = jnp.broadcast_to(tot, CPS.shape)
    me = row * n_col + col
    cps = [rcopy(CPS, CPR.at[me], cp_sem.at[i], dev) for i, dev in enumerate(peers)]
    for cp in cps:
        cp.start()
    CPR[me] = CPS[...]
    run(sta, "Afin")
    run(stb, "Bfin")
    v_out = [pltpu.make_async_copy(VF.at[b], v_hbm.at[pl.ds(b * m, m), :], out_sem.at[NB + b]) for b in range(NB)]
    for cp in v_out:
        cp.start()
    for cp in cps:
        cp.wait()
    total = CPR[0]
    for i in range(1, n_row * n_col):
        total = total + CPR[i]
    cost_ref[...] = total[0:1, 0:cost_ref.shape[1]] / norm
    for cp in u_out + v_out:
        cp.wait()


def solution(mesh):
    n_row = mesh.shape["row"]
    n_col = mesh.shape["col"]

    def local_fn(kern, cost_mat, src_mass, tgt_mass):
        n = kern.shape[0]
        q = src_mass.shape[1]
        m = q // NB
        half = n // 2
        norm = float(n * n_row) * float(kern.shape[1] * n_col)
        dma = pltpu.SemaphoreType.DMA
        any_spec = pl.BlockSpec(memory_space=pl.ANY)
        u, v, cost = pl.pallas_call(
            functools.partial(kernel, n_row, n_col, norm),
            out_shape=(jax.ShapeDtypeStruct((q, n), F32), jax.ShapeDtypeStruct((q, n), F32),
                       jax.ShapeDtypeStruct((1, q), F32)),
            in_specs=[any_spec] * 4,
            out_specs=(any_spec, any_spec, pl.BlockSpec(memory_space=pltpu.VMEM)),
            scratch_shapes=[
                pltpu.VMEM((n, n), BF16), pltpu.VMEM((n, n), BF16),
                pltpu.VMEM((q, n), F32), pltpu.VMEM((q, n), F32),
                pltpu.VMEM((NB, m, n), BF16), pltpu.VMEM((NB, m, n), BF16),
                pltpu.VMEM((NB, m, n), F32), pltpu.VMEM((NB, m, n), F32),
                pltpu.VMEM((NB, m, half), F32), pltpu.VMEM((NB, m, half), F32),
                pltpu.VMEM((NB, m, half), F32), pltpu.VMEM((2, NB, m, half), F32),
                pltpu.VMEM((NB, m, n), F32), pltpu.VMEM((NB, m, n), F32),
                pltpu.VMEM((2, NB, m, n), F32),
                pltpu.VMEM((4, 8, half), F32),
                pltpu.VMEM((128, 128), F32), pltpu.VMEM((8, 128), F32), pltpu.VMEM((n_row * n_col, 8, 128), F32),
                dma((6,)), dma((3,)), dma((2 * NB,)), dma((2, 2)),
                dma((NB, 2)), dma((2, NB, 2, 2)), dma((NB, 2, 2)), dma((NB, 2)),
                dma((NB, NT, 2)), dma((2, NB, NT, 2)), dma((NB, NT, 2)), dma((NB, NT, 2)),
                dma((n_row * n_col - 1, 2)),
            ],
            compiler_params=pltpu.CompilerParams(collective_id=0, has_side_effects=True, vmem_limit_bytes=60 * 1024 * 1024),
        )(kern, cost_mat, src_mass.T, tgt_mass.T)
        return u.T, v.T, cost.reshape(q)

    return jax.shard_map(local_fn, mesh=mesh, in_specs=(P("row", "col"), P("row", "col"), P("row", "prob"), P("col", "prob")),
                         out_specs=(P("row", "prob"), P("col", "prob"), P("prob")), check_vma=False)
```

time: 593 us -> 224 us (0.38)
  waiting for transfers between devices: 441 us -> 0 us
  Pallas kernels: 0 us -> 218 us
  matrix products: 102 us -> 0 us
  blocking collectives: 30.5 us -> 0 us
  between operations: 14.3 us -> 0.64 us
    psum x12 -> x0, waiting for transfers between devices: 441 us -> none  [the longest x6 240 us: local_fn(): tgt_scale = tgt_mass / lax.psum(col_part, 'row')]
    pallas_call x0 -> x1, Pallas kernels: none -> 218 us  [local_fn(): pl.pallas_call(functools.partial(kernel, n_row, n_col, norm), out_shape=(...]
    dot_general x13 -> x0, matrix products: 102 us -> none  [the longest x6 49.9 us: local_fn(): jnp.dot(kernel, tgt_scale.astype(jnp.bfloat16), preferred_element_type=jn...]
    psum x1 -> x0, blocking collectives: 30.5 us -> none  [local_fn(): lax.psum(part_cost, ('row', 'col')) / mass_norm]
  transfers between devices with their start and end apart: 12 -> 0, of which waited for: 12 -> 0; matrix products, arithmetic and copies ran while one was open for 0% -> 0% of each run, Pallas kernels for 0% -> 0%
where the time goes in v1:
time: 224 us
  Pallas kernels  218 us (97%)
  local copies, waits for them, and re-layouts  4.96 us (2%)
    pallas_call x1, Pallas kernels, local_fn(): pl.pallas_call(functools.partial(kernel, n_row, n_col, norm), out_shape=(...  218 us
    unnamed x3, local copies, waits for them, and re-layouts  4.96 us

profile of v1, /device:TPU:0, one launch (start us, length us, event | category | flops | bytes accessed | tf_op | source)
XLA Modules:
  0.0 223.8 jit_solution(11827708309587553442)
XLA Ops:
  0.6 218.2 %shard_map.67 = (f32[64,2304]{1,0:T(8,128)}, f32[64,2304]{1,0:T(8,128)}, f32[1,64]{1,0:T(1,128)}) custom-call(bf16[2304,2304]{1,0:T(8,128)(2,1)} %k_hbm.1, bf16[2304,2304]{1,0:T(8,128)(2,1)} %c_hbm.1, f32[64,2304]{1,0:T(8,128)} %bitcast.5, f32[64,2304]{1,0:T(8,128)} %bitcast.6), custom_call_target="tpu_custom_call" | custom-call | tf_op jit(solution)/shard_map/pallas_call | solution.py:316
  218.8 1.9 copy.10
  220.7 1.9 copy.11
  222.6 1.1 copy.12

commit v2 on v0

v2 whole, which is shorter than its diff:
```python
import functools

import jax
import jax.numpy as jnp
from jax import lax
from jax.experimental import pallas as pl
from jax.experimental.pallas import tpu as pltpu
from jax.sharding import PartitionSpec as P

SWEEPS = 6
MESH = pl.DeviceIdType.MESH
F32 = jnp.float32
BF16 = jnp.bfloat16
NB = 4
T_PIECES = (768, 768, 768)
S_PIECES = (512, 640)


def dot_nn(x, y):
    return jnp.dot(x, y, preferred_element_type=F32)


def spans(sizes):
    out, o = [], 0
    for w in sizes:
        out.append((o, w))
        o += w
    return out


def tiles(size, tile=256):
    return [(o, min(tile, size - o)) for o in range(0, size, tile)]


def kernel(n_row, n_col, norm,
           k_hbm, c_hbm, a_hbm, b_hbm, u_hbm, v_hbm, cost_ref,
           K, KT, C, KCT, A, B, UB, VB, UF, VF, DS, DR, SP, YR, TP, EI, XR, R0, ACC, CPS, CPR,
           k_sem, in_sem, out_sem, r0_sem,
           d_sem, y_sem, u_sem, uf_sem, e_sem, x_sem, v_sem, vf_sem, cp_sem):
    row = lax.axis_index("row")
    col = lax.axis_index("col")
    core = lax.rem(col, 2)
    n = K.shape[0]
    half = n // 2
    m = UB.shape[1]
    total_inst = SWEEPS * NB
    sib = {"col": col + 1 - 2 * core}
    ypeer = {"col": lax.rem(col + 2, n_col)}
    inner = jnp.logical_or(row == 1, row == 2)
    edge = jnp.logical_not(inner)
    zpair = {"row": row + 1 - 2 * lax.rem(row, 2)}
    zmid = {"row": n_row - 1 - row}
    own0 = pl.multiple_of(core * half, 128)
    sib0 = pl.multiple_of((1 - core) * half, 128)
    t_pieces = spans(T_PIECES)
    s_pieces = spans(S_PIECES)

    def at(o, w):
        return pl.ds(pl.multiple_of(o, 128), w)

    def rcopy(src, dst, sem, dev):
        return pltpu.make_async_remote_copy(src_ref=src, dst_ref=dst, send_sem=sem.at[0], recv_sem=sem.at[1],
                                            device_id=dev, device_id_type=MESH)

    rows_per = 384
    per_half = half // rows_per
    k_loads = []
    for h0 in (sib0, own0):
        for j in range(per_half):
            sl = at(h0 + j * rows_per, rows_per)
            cp = pltpu.make_async_copy(k_hbm.at[sl, :], K.at[sl, :], k_sem.at[len(k_loads)])
            cp.start()
            k_loads.append((sl, cp))
    a_load = pltpu.make_async_copy(a_hbm, A, in_sem.at[0])
    b_load = pltpu.make_async_copy(b_hbm, B, in_sem.at[1])
    c_load = pltpu.make_async_copy(c_hbm, C, in_sem.at[2])
    a_load.start()
    b_load.start()
    c_load.start()

    barrier = pltpu.get_barrier_semaphore()
    rel = [(dr, dc) for dr in range(n_row) for dc in range(n_col) if (dr, dc) != (0, 0)]
    peers = [{"row": lax.rem(row + dr, n_row), "col": lax.rem(col + dc, n_col)} for dr, dc in rel]
    for dev in peers:
        pl.semaphore_signal(barrier, inc=1, device_id=dev, device_id_type=MESH)

    ACC[...] = jnp.zeros_like(ACC)

    ones = jnp.ones((16, n), BF16)
    for h in range(2):
        for j in range(per_half):
            sl, cp = k_loads[h * per_half + j]
            cp.wait()

            def turn(t, carry, sl=sl):
                cols = at(t * 256, 256)
                KT[cols, sl] = jnp.transpose(K[sl, cols])
                return carry

            lax.fori_loop(0, n // 256, turn, 0)
            R0[h, :, j * rows_per:(j + 1) * rows_per] = dot_nn(ones, KT[:, sl])[:8]
        if h == 0:
            pl.semaphore_wait(barrier, len(peers))
            r0d = rcopy(R0.at[0], R0.at[2], r0_sem.at[0], sib)
            r0d.start()
    r0d.wait()
    R0[1] = R0[1] + R0[2]
    r0y = rcopy(R0.at[1], R0.at[3], r0_sem.at[1], ypeer)
    r0y.start()
    a_load.wait()
    r0y.wait()
    s0 = R0[1, 0:1] + R0[3, 0:1]

    def u_copy(b, j):
        o, w = s_pieces[j]
        ref = UB.at[b, :, at(own0 + o, w)]
        return rcopy(ref, ref, u_sem.at[b, j], sib)

    def uf_copy(b):
        ref = UF.at[b, :, at(own0, half)]
        return rcopy(ref, ref, uf_sem.at[b], sib)

    for b in range(NB):
        for j, (o, w) in enumerate(s_pieces):
            sl = at(own0 + o, w)
            UB[b, :, sl] = (A[b, :, sl] / s0[:, o:o + w]).astype(BF16)
            u_copy(b, j).start()
    b_load.wait()
    c_load.wait()

    def d_copy(b):
        return rcopy(DS.at[b], DR.at[b], d_sem.at[b], sib)

    def y_copy(par, b, j):
        o, w = s_pieces[j]
        return rcopy(SP.at[b, :, pl.ds(o, w)], YR.at[par, b, :, pl.ds(o, w)], y_sem.at[par, b, j], ypeer)

    def e_copy(b, c):
        o, w = t_pieces[c]
        return rcopy(TP.at[b, :, pl.ds(o, w)], EI.at[b, :, pl.ds(o, w)], e_sem.at[b, c], zpair)

    def x_copy(par, b, c):
        o, w = t_pieces[c]
        return rcopy(TP.at[b, :, pl.ds(o, w)], XR.at[par, b, :, pl.ds(o, w)], x_sem.at[par, b, c], zmid)

    def v_copy(b, c):
        o, w = t_pieces[c]
        ref = VB.at[b, :, pl.ds(o, w)]
        return rcopy(ref, ref, v_sem.at[b, c], zpair)

    def vf_copy(b, c):
        o, w = t_pieces[c]
        ref = VF.at[b, :, pl.ds(o, w)]
        return rcopy(ref, ref, vf_sem.at[b, c], zpair)

    def s1(b, par, last):
        for o, w in tiles(half):
            DS[b, :, o:o + w] = dot_nn(VB[b], KT[:, at(sib0 + o, w)])
        d_copy(b).start()

    def s2(b, par, last):
        for o, w in tiles(half):
            SP[b, :, o:o + w] = dot_nn(VB[b], KT[:, at(own0 + o, w)])

    def v_drain(b):
        @pl.when(inner)
        def _():
            for c in range(len(t_pieces)):
                v_copy(b, c).wait_send()

    def s3(b, par, last):
        d_copy(b).wait_recv()
        for j, (o, w) in enumerate(s_pieces):
            SP[b, :, o:o + w] = SP[b, :, o:o + w] + DR[b, :, o:o + w]
            y_copy(par, b, j).start()
        v_drain(b)

    def s4(j, b, par, last):
        o, w = s_pieces[j]
        y_copy(par, b, j).wait_recv()
        sl = at(own0 + o, w)
        u = A[b, :, sl] / (SP[b, :, o:o + w] + YR[par, b, :, o:o + w])
        UB[b, :, sl] = u.astype(BF16)
        u_copy(b, j).start()
        UF[b, :, sl] = u
        if j == len(s_pieces) - 1:
            pl.when(last)(lambda: uf_copy(b).start())
            d_copy(b).wait_send()
        y_copy(par, b, j).wait_send()

    def t0(b, par, last):
        for j in range(len(s_pieces)):
            u_copy(b, j).wait()

    def t1(c, b, par, last):
        o0, width = t_pieces[c]
        for o, w in tiles(width):
            TP[b, :, o0 + o:o0 + o + w] = dot_nn(UB[b], K[:, o0 + o:o0 + o + w])
        pl.when(edge)(lambda: e_copy(b, c).start())

    def t2(c, b, par, last):
        o, w = t_pieces[c]

        @pl.when(inner)
        def _():
            e_copy(b, c).wait_recv()
            TP[b, :, o:o + w] = TP[b, :, o:o + w] + EI[b, :, o:o + w]
            x_copy(par, b, c).start()

    def t3i(c, b, par, last):
        o, w = t_pieces[c]

        @pl.when(inner)
        def _():
            x_copy(par, b, c).wait_recv()
            v = B[b, :, o:o + w] / (TP[b, :, o:o + w] + XR[par, b, :, o:o + w])
            VB[b, :, o:o + w] = v.astype(BF16)
            v_copy(b, c).start()
            VF[b, :, o:o + w] = v
            pl.when(last)(lambda: vf_copy(b, c).start())
            x_copy(par, b, c).wait_send()

    def t3e(c, b, par, last):
        @pl.when(edge)
        def _():
            v_copy(b, c).wait_recv()
            e_copy(b, c).wait_send()

    def out_copies(b):
        return (pltpu.make_async_copy(UF.at[b], u_hbm.at[b], out_sem.at[b, 0]),
                pltpu.make_async_copy(VF.at[b], v_hbm.at[b], out_sem.at[b, 1]))

    def cost_part(b):
        v_drain(b)
        uf_copy(b).wait()
        acc = jnp.zeros((m, 128), F32)
        for o, w in tiles(n):
            p = UF[b, :, o:o + w] * dot_nn(VB[b], KCT[:, o:o + w])
            for q in range(0, w, 128):
                acc = acc + p[:, q:q + 128]
        ACC[pl.ds(pl.multiple_of(b * m, m), m), :] = acc
        for c in range(len(t_pieces)):
            pl.when(inner)(lambda c=c: vf_copy(b, c).wait_send())
            pl.when(edge)(lambda c=c: vf_copy(b, c).wait_recv())
        for cp in out_copies(b):
            cp.start()

    def kc(t):
        rows = at(t * 128, 128)

        def turn(q, carry):
            cols = at(q * 256, 256)
            KCT[cols, rows] = KT[cols, rows] * jnp.transpose(C[rows, cols])
            return carry

        lax.fori_loop(0, n // 256, turn, 0)

    kc_first = 2

    def tick(i, carry):
        def do(fn, lag, first=0):
            g = i - lag

            @pl.when(jnp.logical_and(g >= first, g < total_inst))
            def _():
                sweep = lax.div(g, NB)
                fn(lax.rem(g, NB), lax.rem(sweep, 2), sweep == SWEEPS - 1)

        part = functools.partial
        do(s1, 0, NB)
        do(s2, 0, NB)
        pl.when(i >= total_inst)(lambda: cost_part(i - total_inst))
        do(part(s4, 0), 1, NB)
        do(part(s4, 1), 1, NB)
        do(part(t3i, 1), 3)
        do(part(t2, 0), 2)
        do(part(t3i, 2), 3)
        do(s3, 0, NB)
        do(part(t2, 1), 2)
        do(t0, 1)
        do(part(t1, 0), 1)
        do(part(t1, 1), 1)
        do(part(t1, 2), 1)
        do(part(t2, 2), 2)
        do(part(t3e, 0), 3)
        do(part(t3e, 1), 3)
        pl.when(jnp.logical_and(i >= kc_first, i < kc_first + n // 128))(lambda: kc(i - kc_first))
        do(part(t3i, 0), 2)
        do(part(t3e, 2), 3)
        return carry

    lax.fori_loop(1, total_inst + NB, tick, 0)

    tot = jnp.sum(jnp.transpose(ACC[...]), axis=0, keepdims=True)
    CPS[...] = jnp.broadcast_to(tot, CPS.shape)
    me = row * n_col + col
    cps = [rcopy(CPS, CPR.at[me], cp_sem.at[i], dev) for i, dev in enumerate(peers)]
    for cp in cps:
        cp.start()
    CPR[me] = CPS[...]
    for cp in cps:
        cp.wait()
    total = CPR[0]
    for i in range(1, n_row * n_col):
        total = total + CPR[i]
    cost_ref[...] = total[0:1, 0:cost_ref.shape[1]] / norm
    for b in range(NB):
        for cp in out_copies(b):
            cp.wait()


def solution(mesh):
    n_row = mesh.shape["row"]
    n_col = mesh.shape["col"]

    def local_fn(kern, cost_mat, src_mass, tgt_mass):
        n = kern.shape[0]
        q = src_mass.shape[1]
        m = q // NB
        half = n // 2
        norm = float(n * n_row) * float(kern.shape[1] * n_col)
        dma = pltpu.SemaphoreType.DMA
        vmem = pltpu.VMEM
        any_spec = pl.BlockSpec(memory_space=pl.ANY)
        np_, ns = len(T_PIECES), len(S_PIECES)
        u, v, cost = pl.pallas_call(
            functools.partial(kernel, n_row, n_col, norm),
            out_shape=(jax.ShapeDtypeStruct((NB, m, n), F32), jax.ShapeDtypeStruct((NB, m, n), F32),
                       jax.ShapeDtypeStruct((1, q), F32)),
            in_specs=[any_spec] * 4,
            out_specs=(any_spec, any_spec, pl.BlockSpec(memory_space=pltpu.VMEM)),
            scratch_shapes=[
                vmem((n, n), BF16), vmem((n, n), BF16), vmem((n, n), BF16), vmem((n, n), BF16),
                vmem((NB, m, n), F32), vmem((NB, m, n), F32),
                vmem((NB, m, n), BF16), vmem((NB, m, n), BF16),
                vmem((NB, m, n), F32), vmem((NB, m, n), F32),
                vmem((NB, m, half), F32), vmem((NB, m, half), F32),
                vmem((NB, m, half), F32), vmem((2, NB, m, half), F32),
                vmem((NB, m, n), F32), vmem((NB, m, n), F32),
                vmem((2, NB, m, n), F32),
                vmem((4, 8, half), F32),
                vmem((128, 128), F32), vmem((8, 128), F32), vmem((n_row * n_col, 8, 128), F32),
                dma((6,)), dma((3,)), dma((NB, 2)), dma((2, 2)),
                dma((NB, 2)), dma((2, NB, ns, 2)), dma((NB, ns, 2)), dma((NB, 2)),
                dma((NB, np_, 2)), dma((2, NB, np_, 2)), dma((NB, np_, 2)), dma((NB, np_, 2)),
                dma((n_row * n_col - 1, 2)),
            ],
            compiler_params=pltpu.CompilerParams(collective_id=0, has_side_effects=True, vmem_limit_bytes=60 * 1024 * 1024),
        )(kern, cost_mat, src_mass.T.reshape(NB, m, n), tgt_mass.T.reshape(NB, m, n))
        return u.reshape(q, n).T, v.reshape(q, n).T, cost.reshape(q)

    return jax.shard_map(local_fn, mesh=mesh, in_specs=(P("row", "col"), P("row", "col"), P("row", "prob"), P("col", "prob")),
                         out_specs=(P("row", "prob"), P("col", "prob"), P("prob")), check_vma=False)
```

time: 593 us -> 169 us (0.28)
  waiting for transfers between devices: 441 us -> 0 us
  Pallas kernels: 0 us -> 163 us
  matrix products: 102 us -> 0 us
  blocking collectives: 30.5 us -> 0 us
  between operations: 14.3 us -> 0.64 us
    psum x12 -> x0, waiting for transfers between devices: 441 us -> none  [the longest x6 240 us: local_fn(): tgt_scale = tgt_mass / lax.psum(col_part, 'row')]
    pallas_call x0 -> x1, Pallas kernels: none -> 163 us  [local_fn(): pl.pallas_call(functools.partial(kernel, n_row, n_col, norm), out_shape=(...]
    dot_general x13 -> x0, matrix products: 102 us -> none  [the longest x6 49.9 us: local_fn(): jnp.dot(kernel, tgt_scale.astype(jnp.bfloat16), preferred_element_type=jn...]
    psum x1 -> x0, blocking collectives: 30.5 us -> none  [local_fn(): lax.psum(part_cost, ('row', 'col')) / mass_norm]
  transfers between devices with their start and end apart: 12 -> 0, of which waited for: 12 -> 0; matrix products, arithmetic and copies ran while one was open for 0% -> 0% of each run, Pallas kernels for 0% -> 0%
where the time goes in v2:
time: 169 us; the launch traced here: 168 us
  Pallas kernels  163 us (96%)
  local copies, waits for them, and re-layouts  4.96 us (3%)
    pallas_call x1, Pallas kernels, local_fn(): pl.pallas_call(functools.partial(kernel, n_row, n_col, norm), out_shape=(...  163 us
    unnamed x3, local copies, waits for them, and re-layouts  4.96 us

profile of v2, /device:TPU:0, one launch (start us, length us, event | category | flops | bytes accessed | tf_op | source)
XLA Modules:
  0.0 168.5 jit_solution(5597676171321441514)
XLA Ops:
  0.6 162.9 %shard_map.67 = (f32[4,16,2304]{2,1,0:T(8,128)}, f32[4,16,2304]{2,1,0:T(8,128)}, f32[1,64]{1,0:T(1,128)}) custom-call(bf16[2304,2304]{1,0:T(8,128)(2,1)} %k_hbm.1, bf16[2304,2304]{1,0:T(8,128)(2,1)} %c_hbm.1, f32[4,16,2304]{2,1,0:T(8,128)} %bitcast.13, f32[4,16,2304]{2,1,0:T(8,128)} %bitcast.14), custom_call_target="tpu_custom_call" | custom-call | tf_op jit(solution)/shard_map/pallas_call | solution.py:326
  163.5 1.9 %copy.10 = f32[2304,64]{0,1:T(8,128)} copy(f32[2304,64]{0,1:T(8,128)} %bitcast.16) | data formatting | bytes 1179648
  165.5 1.9 %copy.11 = f32[2304,64]{0,1:T(8,128)} copy(f32[2304,64]{0,1:T(8,128)} %bitcast.15) | data formatting | bytes 1179648
  167.4 1.1 copy.12

commit v3 on v2

--- a/solution.py
+++ b/solution.py
@@ -12,12 +12,25 @@
 F32 = jnp.float32
 BF16 = jnp.bfloat16
 NB = 4
-T_PIECES = (768, 768, 768)
+T_PIECES = (512, 512, 512, 512, 256)
+EARLY = 3
 S_PIECES = (512, 640)
+KC_FIRST = 5
+ORDER = (
+    ("e", 4, 4), ("t2", 4, 3), ("s4", 0, 1), ("t2", 3, 3), ("e", 3, 4), ("s1", None, 0), ("t3", 0, 3),
+    ("s2", None, 0), ("s4", 1, 1), ("ta", None, 1), ("s3", 0, 0), ("t3", 1, 3), ("t0", None, 1), ("t1", 0, 1),
+    ("t2", 0, 2), ("s3", 1, 0), ("t1", 1, 1), ("t3", 2, 3), ("t1", 2, 1), ("kc", None, 0), ("e", 0, 3),
+    ("t2", 1, 2), ("t1", 3, 1), ("t2", 2, 2), ("kt", None, 0), ("t3", 4, 3), ("t3", 3, 3), ("cost", None, 0),
+    ("e", 1, 3), ("t1", 4, 1), ("e", 2, 3), ("sa", None, -1),
+)
 
 
 def dot_nn(x, y):
     return jnp.dot(x, y, preferred_element_type=F32)
+
+
+def dot_nt(x, y):
+    return lax.dot_general(x, y, (((1,), (1,)), ((), ())), preferred_element_type=F32)
 
 
 def spans(sizes):
@@ -64,6 +77,9 @@
 
     rows_per = 384
     per_half = half // rows_per
+    a_load = pltpu.make_async_copy(a_hbm, A, in_sem.at[0])
+    b_load = pltpu.make_async_copy(b_hbm, B, in_sem.at[1])
+    c_load = pltpu.make_async_copy(c_hbm, C, in_sem.at[2])
     k_loads = []
     for h0 in (sib0, own0):
         for j in range(per_half):
@@ -71,12 +87,7 @@
             cp = pltpu.make_async_copy(k_hbm.at[sl, :], K.at[sl, :], k_sem.at[len(k_loads)])
             cp.start()
             k_loads.append((sl, cp))
-    a_load = pltpu.make_async_copy(a_hbm, A, in_sem.at[0])
-    b_load = pltpu.make_async_copy(b_hbm, B, in_sem.at[1])
-    c_load = pltpu.make_async_copy(c_hbm, C, in_sem.at[2])
     a_load.start()
-    b_load.start()
-    c_load.start()
 
     barrier = pltpu.get_barrier_semaphore()
     rel = [(dr, dc) for dr in range(n_row) for dc in range(n_col) if (dr, dc) != (0, 0)]
@@ -91,18 +102,13 @@
         for j in range(per_half):
             sl, cp = k_loads[h * per_half + j]
             cp.wait()
-
-            def turn(t, carry, sl=sl):
-                cols = at(t * 256, 256)
-                KT[cols, sl] = jnp.transpose(K[sl, cols])
-                return carry
-
-            lax.fori_loop(0, n // 256, turn, 0)
-            R0[h, :, j * rows_per:(j + 1) * rows_per] = dot_nn(ones, KT[:, sl])[:8]
+            R0[h, :, j * rows_per:(j + 1) * rows_per] = dot_nt(ones, K[sl, :])[:8]
         if h == 0:
             pl.semaphore_wait(barrier, len(peers))
             r0d = rcopy(R0.at[0], R0.at[2], r0_sem.at[0], sib)
             r0d.start()
+    b_load.start()
+    c_load.start()
     r0d.wait()
     R0[1] = R0[1] + R0[2]
     r0y = rcopy(R0.at[1], R0.at[3], r0_sem.at[1], ypeer)
@@ -126,10 +132,10 @@
             UB[b, :, sl] = (A[b, :, sl] / s0[:, o:o + w]).astype(BF16)
             u_copy(b, j).start()
     b_load.wait()
-    c_load.wait()
-
-    def d_copy(b):
-        return rcopy(DS.at[b], DR.at[b], d_sem.at[b], sib)
+
+    def d_copy(b, j):
+        o, w = s_pieces[j]
+        return rcopy(DS.at[b, :, pl.ds(o, w)], DR.at[b, :, pl.ds(o, w)], d_sem.at[b, j], sib)
 
     def y_copy(par, b, j):
         o, w = s_pieces[j]
@@ -153,14 +159,23 @@
         ref = VF.at[b, :, pl.ds(o, w)]
         return rcopy(ref, ref, vf_sem.at[b, c], zpair)
 
+    early = sum(T_PIECES[:EARLY])
+
+    def sa(b, par, last):
+        for dst, h0 in ((DS, sib0), (SP, own0)):
+            for o, w in tiles(half):
+                dst[b, :, o:o + w] = dot_nn(VB[b, :, :early], KT[:early, at(h0 + o, w)])
+
     def s1(b, par, last):
-        for o, w in tiles(half):
-            DS[b, :, o:o + w] = dot_nn(VB[b], KT[:, at(sib0 + o, w)])
-        d_copy(b).start()
+        for j, (o0, width) in enumerate(s_pieces):
+            for o, w in tiles(width):
+                o += o0
+                DS[b, :, o:o + w] += dot_nn(VB[b, :, early:], KT[early:, at(sib0 + o, w)])
+            d_copy(b, j).start()
 
     def s2(b, par, last):
         for o, w in tiles(half):
-            SP[b, :, o:o + w] = dot_nn(VB[b], KT[:, at(own0 + o, w)])
+            SP[b, :, o:o + w] += dot_nn(VB[b, :, early:], KT[early:, at(own0 + o, w)])
 
     def v_drain(b):
         @pl.when(inner)
@@ -168,12 +183,13 @@
             for c in range(len(t_pieces)):
                 v_copy(b, c).wait_send()
 
-    def s3(b, par, last):
-        d_copy(b).wait_recv()
-        for j, (o, w) in enumerate(s_pieces):
-            SP[b, :, o:o + w] = SP[b, :, o:o + w] + DR[b, :, o:o + w]
-            y_copy(par, b, j).start()
-        v_drain(b)
+    def s3(j, b, par, last):
+        o, w = s_pieces[j]
+        d_copy(b, j).wait_recv()
+        SP[b, :, o:o + w] = SP[b, :, o:o + w] + DR[b, :, o:o + w]
+        y_copy(par, b, j).start()
+        if j == len(s_pieces) - 1:
+            v_drain(b)
 
     def s4(j, b, par, last):
         o, w = s_pieces[j]
@@ -185,17 +201,22 @@
         UF[b, :, sl] = u
         if j == len(s_pieces) - 1:
             pl.when(last)(lambda: uf_copy(b).start())
-            d_copy(b).wait_send()
+        d_copy(b, j).wait_send()
         y_copy(par, b, j).wait_send()
 
     def t0(b, par, last):
         for j in range(len(s_pieces)):
             u_copy(b, j).wait()
 
+    def ta(b, par, last):
+        for o, w in tiles(n):
+            TP[b, :, o:o + w] = dot_nn(UB[b, :, at(own0, half)], K[at(own0, half), o:o + w])
+
     def t1(c, b, par, last):
         o0, width = t_pieces[c]
         for o, w in tiles(width):
-            TP[b, :, o0 + o:o0 + o + w] = dot_nn(UB[b], K[:, o0 + o:o0 + o + w])
+            o += o0
+            TP[b, :, o:o + w] += dot_nn(UB[b, :, at(sib0, half)], K[at(sib0, half), o:o + w])
         pl.when(edge)(lambda: e_copy(b, c).start())
 
     def t2(c, b, par, last):
@@ -255,38 +276,35 @@
 
         lax.fori_loop(0, n // 256, turn, 0)
 
-    kc_first = 2
+    def kt(t):
+        rows = at(t * (n // 3), n // 3)
+
+        def turn(q, carry):
+            cols = at(q * 256, 256)
+            KT[cols, rows] = jnp.transpose(K[rows, cols])
+            return carry
+
+        lax.fori_loop(0, n // 256, turn, 0)
+
+    steps = {"sa": sa, "s1": s1, "s2": s2, "s3": s3, "s4": s4, "ta": ta, "t0": t0, "t1": t1, "t2": t2, "t3": t3i, "e": t3e}
 
     def tick(i, carry):
-        def do(fn, lag, first=0):
-            g = i - lag
-
-            @pl.when(jnp.logical_and(g >= first, g < total_inst))
-            def _():
-                sweep = lax.div(g, NB)
-                fn(lax.rem(g, NB), lax.rem(sweep, 2), sweep == SWEEPS - 1)
-
-        part = functools.partial
-        do(s1, 0, NB)
-        do(s2, 0, NB)
-        pl.when(i >= total_inst)(lambda: cost_part(i - total_inst))
-        do(part(s4, 0), 1, NB)
-        do(part(s4, 1), 1, NB)
-        do(part(t3i, 1), 3)
-        do(part(t2, 0), 2)
-        do(part(t3i, 2), 3)
-        do(s3, 0, NB)
-        do(part(t2, 1), 2)
-        do(t0, 1)
-        do(part(t1, 0), 1)
-        do(part(t1, 1), 1)
-        do(part(t1, 2), 1)
-        do(part(t2, 2), 2)
-        do(part(t3e, 0), 3)
-        do(part(t3e, 1), 3)
-        pl.when(jnp.logical_and(i >= kc_first, i < kc_first + n // 128))(lambda: kc(i - kc_first))
-        do(part(t3i, 0), 2)
-        do(part(t3e, 2), 3)
+        for name, piece, lag in ORDER:
+            if name == "cost":
+                pl.when(i >= total_inst)(lambda: cost_part(i - total_inst))
+            elif name == "kt":
+                pl.when(i < 4)(lambda: kt(i - 1))
+            elif name == "kc":
+                pl.when(i == KC_FIRST)(lambda: c_load.wait())
+                pl.when(jnp.logical_and(i >= KC_FIRST, i < KC_FIRST + n // 128))(lambda: kc(i - KC_FIRST))
+            else:
+                g = i - lag
+                fn = steps[name] if piece is None else functools.partial(steps[name], piece)
+
+                @pl.when(jnp.logical_and(g >= (NB if name[0] == "s" else 0), g < total_inst))
+                def _():
+                    sweep = lax.div(g, NB)
+                    fn(lax.rem(g, NB), lax.rem(sweep, 2), sweep == SWEEPS - 1)
         return carry
 
     lax.fori_loop(1, total_inst + NB, tick, 0)
@@ -341,7 +359,7 @@
                 vmem((4, 8, half), F32),
                 vmem((128, 128), F32), vmem((8, 128), F32), vmem((n_row * n_col, 8, 128), F32),
                 dma((6,)), dma((3,)), dma((NB, 2)), dma((2, 2)),
-                dma((NB, 2)), dma((2, NB, ns, 2)), dma((NB, ns, 2)), dma((NB, 2)),
+                dma((NB, ns, 2)), dma((2, NB, ns, 2)), dma((NB, ns, 2)), dma((NB, 2)),
                 dma((NB, np_, 2)), dma((2, NB, np_, 2)), dma((NB, np_, 2)), dma((NB, np_, 2)),
                 dma((n_row * n_col - 1, 2)),
             ],

time: 169 us -> 157 us (0.929)
  Pallas kernels: 163 us -> 151 us
    pallas_call x1, Pallas kernels: 163 us -> 151 us  [local_fn(): pl.pallas_call(functools.partial(kernel, n_row, n_col, norm), out_shape=(...]
where the time goes in v3:
time: 157 us
  Pallas kernels  151 us (96%)
  local copies, waits for them, and re-layouts  4.96 us (3%)
    pallas_call x1, Pallas kernels, local_fn(): pl.pallas_call(functools.partial(kernel, n_row, n_col, norm), out_shape=(...  151 us
    unnamed x3, local copies, waits for them, and re-layouts  4.96 us

profile of v3, /device:TPU:0, one launch (start us, length us, event | category | flops | bytes accessed | tf_op | source)
XLA Modules:
  0.0 157.0 jit_solution(8779139391175712332)
XLA Ops:
  0.6 151.4 %shard_map.67 = (f32[4,16,2304]{2,1,0:T(8,128)}, f32[4,16,2304]{2,1,0:T(8,128)}, f32[1,64]{1,0:T(1,128)}) custom-call(bf16[2304,2304]{1,0:T(8,128)(2,1)} %k_hbm.1, bf16[2304,2304]{1,0:T(8,128)(2,1)} %c_hbm.1, f32[4,16,2304]{2,1,0:T(8,128)} %bitcast.13, f32[4,16,2304]{2,1,0:T(8,128)} %bitcast.14), custom_call_target="tpu_custom_call" | custom-call | tf_op jit(solution)/shard_map/pallas_call | solution.py:344
  152.1 1.9 %copy.10 = f32[2304,64]{0,1:T(8,128)} copy(f32[2304,64]{0,1:T(8,128)} %bitcast.16) | data formatting | bytes 1179648
  154.0 1.9 %copy.11 = f32[2304,64]{0,1:T(8,128)} copy(f32[2304,64]{0,1:T(8,128)} %bitcast.15) | data formatting | bytes 1179648
  155.9 1.1 copy.12

commit v4 on v3

--- a/solution.py
+++ b/solution.py
@@ -15,13 +15,14 @@
 T_PIECES = (512, 512, 512, 512, 256)
 EARLY = 3
 S_PIECES = (512, 640)
+K_PIECES = (768, 768, 512, 256)
 KC_FIRST = 5
 ORDER = (
     ("e", 4, 4), ("t2", 4, 3), ("s4", 0, 1), ("t2", 3, 3), ("e", 3, 4), ("s1", None, 0), ("t3", 0, 3),
-    ("s2", None, 0), ("s4", 1, 1), ("ta", None, 1), ("s3", 0, 0), ("t3", 1, 3), ("t0", None, 1), ("t1", 0, 1),
-    ("t2", 0, 2), ("s3", 1, 0), ("t1", 1, 1), ("t3", 2, 3), ("t1", 2, 1), ("kc", None, 0), ("e", 0, 3),
-    ("t2", 1, 2), ("t1", 3, 1), ("t2", 2, 2), ("kt", None, 0), ("t3", 4, 3), ("t3", 3, 3), ("cost", None, 0),
-    ("e", 1, 3), ("t1", 4, 1), ("e", 2, 3), ("sa", None, -1),
+    ("s2", None, 0), ("cost", None, 0), ("s4", 1, 1), ("ta", None, 1), ("s3", 0, 0), ("t3", 1, 3),
+    ("t0", None, 1), ("t1", 0, 1), ("t2", 0, 2), ("s3", 1, 0), ("t1", 1, 1), ("t3", 2, 3), ("t1", 2, 1),
+    ("kc", None, 0), ("e", 0, 3), ("t2", 1, 2), ("t1", 3, 1), ("t2", 2, 2), ("kt", None, 0), ("t3", 4, 3),
+    ("t3", 3, 3), ("e", 1, 3), ("t1", 4, 1), ("e", 2, 3), ("sa", None, -1), ("ca", None, -1),
 )
 
 
@@ -46,9 +47,9 @@
 
 
 def kernel(n_row, n_col, norm,
-           k_hbm, c_hbm, a_hbm, b_hbm, u_hbm, v_hbm, cost_ref,
-           K, KT, C, KCT, A, B, UB, VB, UF, VF, DS, DR, SP, YR, TP, EI, XR, R0, ACC, CPS, CPR,
-           k_sem, in_sem, out_sem, r0_sem,
+           k_hbm, c_hbm, a_hbm, b_hbm, UF, VF, cost_ref,
+           K, KT, C, KCT, A, B, UB, VB, WP, DS, DR, SP, YR, TP, EI, XR, RX, ACC, CPS, CPR,
+           k_sem, in_sem, r_sem,
            d_sem, y_sem, u_sem, uf_sem, e_sem, x_sem, v_sem, vf_sem, cp_sem):
     row = lax.axis_index("row")
     col = lax.axis_index("col")
@@ -75,18 +76,13 @@
         return pltpu.make_async_remote_copy(src_ref=src, dst_ref=dst, send_sem=sem.at[0], recv_sem=sem.at[1],
                                             device_id=dev, device_id_type=MESH)
 
-    rows_per = 384
-    per_half = half // rows_per
     a_load = pltpu.make_async_copy(a_hbm, A, in_sem.at[0])
     b_load = pltpu.make_async_copy(b_hbm, B, in_sem.at[1])
     c_load = pltpu.make_async_copy(c_hbm, C, in_sem.at[2])
-    k_loads = []
-    for h0 in (sib0, own0):
-        for j in range(per_half):
-            sl = at(h0 + j * rows_per, rows_per)
-            cp = pltpu.make_async_copy(k_hbm.at[sl, :], K.at[sl, :], k_sem.at[len(k_loads)])
-            cp.start()
-            k_loads.append((sl, cp))
+    k_loads = [pltpu.make_async_copy(k_hbm.at[o:o + w, :], K.at[o:o + w, :], k_sem.at[j])
+               for j, (o, w) in enumerate(spans(K_PIECES))]
+    for cp in k_loads:
+        cp.start()
     a_load.start()
 
     barrier = pltpu.get_barrier_semaphore()
@@ -98,24 +94,24 @@
     ACC[...] = jnp.zeros_like(ACC)
 
     ones = jnp.ones((16, n), BF16)
-    for h in range(2):
-        for j in range(per_half):
-            sl, cp = k_loads[h * per_half + j]
-            cp.wait()
-            R0[h, :, j * rows_per:(j + 1) * rows_per] = dot_nt(ones, K[sl, :])[:8]
-        if h == 0:
-            pl.semaphore_wait(barrier, len(peers))
-            r0d = rcopy(R0.at[0], R0.at[2], r0_sem.at[0], sib)
-            r0d.start()
+    for cp, (o, w) in zip(k_loads, spans(K_PIECES)):
+        cp.wait()
+        RX[col, :, o:o + w] = dot_nt(ones, K[o:o + w, :])[:1]
+    pl.semaphore_wait(barrier, len(peers))
+    r_copies = [rcopy(RX.at[col], RX.at[col], r_sem.at[d - 1], {"col": lax.rem(col + d, n_col)}) for d in range(1, n_col)]
+    for cp in r_copies:
+        cp.start()
     b_load.start()
     c_load.start()
-    r0d.wait()
-    R0[1] = R0[1] + R0[2]
-    r0y = rcopy(R0.at[1], R0.at[3], r0_sem.at[1], ypeer)
-    r0y.start()
     a_load.wait()
-    r0y.wait()
-    s0 = R0[1, 0:1] + R0[3, 0:1]
+    for cp in r_copies:
+        cp.wait()
+    s0 = RX[0] + RX[1]
+    for d in range(2, n_col):
+        s0 = s0 + RX[d]
+    for b in range(NB):
+        UB[b] = (A[b] / s0).astype(BF16)
+    b_load.wait()
 
     def u_copy(b, j):
         o, w = s_pieces[j]
@@ -125,13 +121,6 @@
     def uf_copy(b):
         ref = UF.at[b, :, at(own0, half)]
         return rcopy(ref, ref, uf_sem.at[b], sib)
-
-    for b in range(NB):
-        for j, (o, w) in enumerate(s_pieces):
-            sl = at(own0 + o, w)
-            UB[b, :, sl] = (A[b, :, sl] / s0[:, o:o + w]).astype(BF16)
-            u_copy(b, j).start()
-    b_load.wait()
 
     def d_copy(b, j):
         o, w = s_pieces[j]
@@ -247,24 +236,22 @@
             v_copy(b, c).wait_recv()
             e_copy(b, c).wait_send()
 
-    def out_copies(b):
-        return (pltpu.make_async_copy(UF.at[b], u_hbm.at[b], out_sem.at[b, 0]),
-                pltpu.make_async_copy(VF.at[b], v_hbm.at[b], out_sem.at[b, 1]))
+    def cost_early(b):
+        for o, w in tiles(n):
+            WP[:, o:o + w] = dot_nn(VB[b, :, :early], KCT[:early, o:o + w])
 
     def cost_part(b):
         v_drain(b)
         uf_copy(b).wait()
         acc = jnp.zeros((m, 128), F32)
         for o, w in tiles(n):
-            p = UF[b, :, o:o + w] * dot_nn(VB[b], KCT[:, o:o + w])
+            p = UF[b, :, o:o + w] * (WP[:, o:o + w] + dot_nn(VB[b, :, early:], KCT[early:, o:o + w]))
             for q in range(0, w, 128):
                 acc = acc + p[:, q:q + 128]
         ACC[pl.ds(pl.multiple_of(b * m, m), m), :] = acc
         for c in range(len(t_pieces)):
             pl.when(inner)(lambda c=c: vf_copy(b, c).wait_send())
             pl.when(edge)(lambda c=c: vf_copy(b, c).wait_recv())
-        for cp in out_copies(b):
-            cp.start()
 
     def kc(t):
         rows = at(t * 128, 128)
@@ -292,6 +279,9 @@
         for name, piece, lag in ORDER:
             if name == "cost":
                 pl.when(i >= total_inst)(lambda: cost_part(i - total_inst))
+            elif name == "ca":
+                g = i - lag
+                pl.when(jnp.logical_and(g >= total_inst, g < total_inst + NB))(lambda: cost_early(g - total_inst))
             elif name == "kt":
                 pl.when(i < 4)(lambda: kt(i - 1))
             elif name == "kc":
@@ -301,7 +291,7 @@
                 g = i - lag
                 fn = steps[name] if piece is None else functools.partial(steps[name], piece)
 
-                @pl.when(jnp.logical_and(g >= (NB if name[0] == "s" else 0), g < total_inst))
+                @pl.when(jnp.logical_and(g >= (NB if name[0] == "s" or name == "t0" else 0), g < total_inst))
                 def _():
                     sweep = lax.div(g, NB)
                     fn(lax.rem(g, NB), lax.rem(sweep, 2), sweep == SWEEPS - 1)
@@ -322,9 +312,6 @@
     for i in range(1, n_row * n_col):
         total = total + CPR[i]
     cost_ref[...] = total[0:1, 0:cost_ref.shape[1]] / norm
-    for b in range(NB):
-        for cp in out_copies(b):
-            cp.wait()
 
 
 def solution(mesh):
@@ -343,22 +330,21 @@
         np_, ns = len(T_PIECES), len(S_PIECES)
         u, v, cost = pl.pallas_call(
             functools.partial(kernel, n_row, n_col, norm),
-            out_shape=(jax.ShapeDtypeStruct((NB, m, n), F32), jax.ShapeDtypeStruct((NB, m, n), F32),
-                       jax.ShapeDtypeStruct((1, q), F32)),
+            out_shape=(vmem((NB, m, n), F32), vmem((NB, m, n), F32), vmem((1, q), F32)),
             in_specs=[any_spec] * 4,
-            out_specs=(any_spec, any_spec, pl.BlockSpec(memory_space=pltpu.VMEM)),
+            out_specs=(pl.BlockSpec(memory_space=vmem),) * 3,
             scratch_shapes=[
                 vmem((n, n), BF16), vmem((n, n), BF16), vmem((n, n), BF16), vmem((n, n), BF16),
                 vmem((NB, m, n), F32), vmem((NB, m, n), F32),
                 vmem((NB, m, n), BF16), vmem((NB, m, n), BF16),
-                vmem((NB, m, n), F32), vmem((NB, m, n), F32),
+                vmem((m, n), F32),
                 vmem((NB, m, half), F32), vmem((NB, m, half), F32),
                 vmem((NB, m, half), F32), vmem((2, NB, m, half), F32),
                 vmem((NB, m, n), F32), vmem((NB, m, n), F32),
                 vmem((2, NB, m, n), F32),
-                vmem((4, 8, half), F32),
+                vmem((n_col, 1, n), F32),
                 vmem((128, 128), F32), vmem((8, 128), F32), vmem((n_row * n_col, 8, 128), F32),
-                dma((6,)), dma((3,)), dma((NB, 2)), dma((2, 2)),
+                dma((len(K_PIECES),)), dma((3,)), dma((n_col - 1, 2)),
                 dma((NB, ns, 2)), dma((2, NB, ns, 2)), dma((NB, ns, 2)), dma((NB, 2)),
                 dma((NB, np_, 2)), dma((2, NB, np_, 2)), dma((NB, np_, 2)), dma((NB, np_, 2)),
                 dma((n_row * n_col - 1, 2)),

time: 157 us -> 154 us (0.981)
  local copies, waits for them, and re-layouts: 4.96 us -> 2.14 us
    unnamed x3, local copies, waits for them, and re-layouts: 4.96 us -> 2.14 us
where the time goes in v4:
time: 154 us
  Pallas kernels  151 us (98%)
  local copies, waits for them, and re-layouts  2.14 us (1%)
    pallas_call x1, Pallas kernels, local_fn(): pl.pallas_call(functools.partial(kernel, n_row, n_col, norm), out_shape=(...  151 us

profile of v4, /device:TPU:0, one launch (start us, length us, event | category | flops | bytes accessed | tf_op | source)
XLA Modules:
  0.0 153.5 jit_solution(14915135238749786687)
XLA Ops:
  0.6 150.8 %shard_map.67 = (f32[4,16,2304]{2,1,0:T(8,128)S(1)}, f32[4,16,2304]{2,1,0:T(8,128)S(1)}, f32[1,64]{1,0:T(1,128)S(1)}) custom-call(bf16[2304,2304]{1,0:T(8,128)(2,1)} %k_hbm.1, bf16[2304,2304]{1,0:T(8,128)(2,1)} %c_hbm.1, f32[4,16,2304]{2,1,0:T(8,128)} %bitcast.16, f32[4,16,2304]{2,1,0:T(8,128)} %bitcast.17), custom_call_target="tpu_custom_call" | custom-call | tf_op jit(solution)/shard_map/pallas_call | solution.py:331
  151.4 0.8 copy.10
  152.2 0.8 copy.11
  153.0 0.5 copy.12

commit v5 on v4

--- a/solution.py
+++ b/solution.py
@@ -13,16 +13,18 @@
 BF16 = jnp.bfloat16
 NB = 4
 T_PIECES = (512, 512, 512, 512, 256)
-EARLY = 3
+EARLY = ((0, 1), (2,))
+TA_PIECES = (1024, 1280)
 S_PIECES = (512, 640)
 K_PIECES = (768, 768, 512, 256)
 KC_FIRST = 5
 ORDER = (
-    ("e", 4, 4), ("t2", 4, 3), ("s4", 0, 1), ("t2", 3, 3), ("e", 3, 4), ("s1", None, 0), ("t3", 0, 3),
-    ("s2", None, 0), ("cost", None, 0), ("s4", 1, 1), ("ta", None, 1), ("s3", 0, 0), ("t3", 1, 3),
-    ("t0", None, 1), ("t1", 0, 1), ("t2", 0, 2), ("s3", 1, 0), ("t1", 1, 1), ("t3", 2, 3), ("t1", 2, 1),
-    ("kc", None, 0), ("e", 0, 3), ("t2", 1, 2), ("t1", 3, 1), ("t2", 2, 2), ("kt", None, 0), ("t3", 4, 3),
-    ("t3", 3, 3), ("e", 1, 3), ("t1", 4, 1), ("e", 2, 3), ("sa", None, -1), ("ca", None, -1),
+    ("s4", 0, 1), ("t3", 1, 3), ("s4", 1, 1), ("ta", 0, 1), ("t2", 0, 2), ("t3", 2, 3), ("s3", 0, 0),
+    ("ta", 1, 1), ("s3", 1, 0), ("t2", 1, 2), ("t3", 3, 3), ("t0", None, 1), ("t1", 0, 1), ("t3", 4, 3),
+    ("t1", 1, 1), ("t2", 2, 2), ("kc", None, 0), ("t1", 2, 1), ("t2", 3, 2), ("t1", 3, 1), ("e", 0, 3),
+    ("t2", 4, 2), ("kt", None, 0), ("e", 1, 3), ("sa", 0, -1), ("e", 2, 3), ("sa", 1, -1), ("ca", None, -1),
+    ("t3", 0, 2), ("e", 3, 3), ("t1", 4, 1), ("e", 4, 3), ("s1", None, -1), ("s2", None, -1),
+    ("cost", None, -1),
 )
 
 
@@ -148,12 +150,15 @@
         ref = VF.at[b, :, pl.ds(o, w)]
         return rcopy(ref, ref, vf_sem.at[b, c], zpair)
 
-    early = sum(T_PIECES[:EARLY])
-
-    def sa(b, par, last):
+    early_spans = spans([sum(T_PIECES[c] for c in group) for group in EARLY])
+    early = sum(w for _, w in early_spans)
+
+    def sa(q, b, par, last):
+        k0, kw = early_spans[q]
         for dst, h0 in ((DS, sib0), (SP, own0)):
             for o, w in tiles(half):
-                dst[b, :, o:o + w] = dot_nn(VB[b, :, :early], KT[:early, at(h0 + o, w)])
+                part = dot_nn(VB[b, :, k0:k0 + kw], KT[k0:k0 + kw, at(h0 + o, w)])
+                dst[b, :, o:o + w] = part if q == 0 else dst[b, :, o:o + w] + part
 
     def s1(b, par, last):
         for j, (o0, width) in enumerate(s_pieces):
@@ -197,8 +202,10 @@
         for j in range(len(s_pieces)):
             u_copy(b, j).wait()
 
-    def ta(b, par, last):
-        for o, w in tiles(n):
+    def ta(q, b, par, last):
+        o0, width = spans(TA_PIECES)[q]
+        for o, w in tiles(width):
+            o += o0
             TP[b, :, o:o + w] = dot_nn(UB[b, :, at(own0, half)], K[at(own0, half), o:o + w])
 
     def t1(c, b, par, last):
@@ -278,7 +285,8 @@
     def tick(i, carry):
         for name, piece, lag in ORDER:
             if name == "cost":
-                pl.when(i >= total_inst)(lambda: cost_part(i - total_inst))
+                g = i - lag
+                pl.when(jnp.logical_and(g >= total_inst, g < total_inst + NB))(lambda: cost_part(g - total_inst))
             elif name == "ca":
                 g = i - lag
                 pl.when(jnp.logical_and(g >= total_inst, g < total_inst + NB))(lambda: cost_early(g - total_inst))

time: 154 us -> 156 us (1.013)
  Pallas kernels: 151 us -> 153 us
    pallas_call x1, Pallas kernels: 151 us -> 153 us  [local_fn(): pl.pallas_call(functools.partial(kernel, n_row, n_col, norm), out_shape=(...]
where the time goes in v5:
time: 156 us
  Pallas kernels  153 us (98%)
  local copies, waits for them, and re-layouts  2.14 us (1%)
    pallas_call x1, Pallas kernels, local_fn(): pl.pallas_call(functools.partial(kernel, n_row, n_col, norm), out_shape=(...  153 us

profile of v5, /device:TPU:0, one launch (start us, length us, event | category | flops | bytes accessed | tf_op | source)
XLA Modules:
  0.0 155.9 jit_solution(12739523726939867149)
XLA Ops:
  0.6 153.1 %shard_map.67 = (f32[4,16,2304]{2,1,0:T(8,128)S(1)}, f32[4,16,2304]{2,1,0:T(8,128)S(1)}, f32[1,64]{1,0:T(1,128)S(1)}) custom-call(bf16[2304,2304]{1,0:T(8,128)(2,1)} %k_hbm.1, bf16[2304,2304]{1,0:T(8,128)(2,1)} %c_hbm.1, f32[4,16,2304]{2,1,0:T(8,128)} %bitcast.16, f32[4,16,2304]{2,1,0:T(8,128)} %bitcast.17), custom_call_target="tpu_custom_call" | custom-call | tf_op jit(solution)/shard_map/pallas_call | solution.py:339
  153.8 0.8 copy.10
  154.6 0.8 copy.11
  155.4 0.5 copy.12

commit v6 on v5

--- a/solution.py
+++ b/solution.py
@@ -13,18 +13,16 @@
 BF16 = jnp.bfloat16
 NB = 4
 T_PIECES = (512, 512, 512, 512, 256)
-EARLY = ((0, 1), (2,))
-TA_PIECES = (1024, 1280)
+EARLY = ((0, 1, 2),)
+TA_PIECES = (2304,)
 S_PIECES = (512, 640)
 K_PIECES = (768, 768, 512, 256)
 KC_FIRST = 5
 ORDER = (
-    ("s4", 0, 1), ("t3", 1, 3), ("s4", 1, 1), ("ta", 0, 1), ("t2", 0, 2), ("t3", 2, 3), ("s3", 0, 0),
-    ("ta", 1, 1), ("s3", 1, 0), ("t2", 1, 2), ("t3", 3, 3), ("t0", None, 1), ("t1", 0, 1), ("t3", 4, 3),
-    ("t1", 1, 1), ("t2", 2, 2), ("kc", None, 0), ("t1", 2, 1), ("t2", 3, 2), ("t1", 3, 1), ("e", 0, 3),
-    ("t2", 4, 2), ("kt", None, 0), ("e", 1, 3), ("sa", 0, -1), ("e", 2, 3), ("sa", 1, -1), ("ca", None, -1),
-    ("t3", 0, 2), ("e", 3, 3), ("t1", 4, 1), ("e", 4, 3), ("s1", None, -1), ("s2", None, -1),
-    ("cost", None, -1),
+    ("e", 1, 4), ("e", 2, 4), ("sa", 0, 0), ("ca", None, 0), ("e", 3, 4), ("t3", 0, 3), ("s4", 0, 1),
+    ("e", 4, 4), ("s1", None, 0), ("cost", None, 0), ("t3", 1, 3), ("s4", 1, 1), ("ta", 0, 1), ("s3", 0, 0),
+    ("t2", 0, 2), ("s3", 1, 0), ("t3", 2, 3), ("t2", 1, 2), ("t0", None, 1), ("t1", None, 1), ("t3", 3, 3),
+    ("t2", 2, 2), ("t3", 4, 3), ("e", 0, 3), ("kc", None, 0), ("t2", 3, 2), ("t2", 4, 2), ("kt", None, 0),
 )
 
 
@@ -166,8 +164,6 @@
                 o += o0
                 DS[b, :, o:o + w] += dot_nn(VB[b, :, early:], KT[early:, at(sib0 + o, w)])
             d_copy(b, j).start()
-
-    def s2(b, par, last):
         for o, w in tiles(half):
             SP[b, :, o:o + w] += dot_nn(VB[b, :, early:], KT[early:, at(own0 + o, w)])
 
@@ -208,12 +204,17 @@
             o += o0
             TP[b, :, o:o + w] = dot_nn(UB[b, :, at(own0, half)], K[at(own0, half), o:o + w])
 
-    def t1(c, b, par, last):
-        o0, width = t_pieces[c]
-        for o, w in tiles(width):
-            o += o0
-            TP[b, :, o:o + w] += dot_nn(UB[b, :, at(sib0, half)], K[at(sib0, half), o:o + w])
-        pl.when(edge)(lambda: e_copy(b, c).start())
+    def t1(b, par, last):
+        def products(send):
+            for c, (o0, width) in enumerate(t_pieces):
+                for o, w in tiles(width):
+                    o += o0
+                    TP[b, :, o:o + w] += dot_nn(UB[b, :, at(sib0, half)], K[at(sib0, half), o:o + w])
+                if send:
+                    e_copy(b, c).start()
+
+        pl.when(edge)(lambda: products(True))
+        pl.when(inner)(lambda: products(False))
 
     def t2(c, b, par, last):
         o, w = t_pieces[c]
@@ -280,7 +281,7 @@
 
         lax.fori_loop(0, n // 256, turn, 0)
 
-    steps = {"sa": sa, "s1": s1, "s2": s2, "s3": s3, "s4": s4, "ta": ta, "t0": t0, "t1": t1, "t2": t2, "t3": t3i, "e": t3e}
+    steps = {"sa": sa, "s1": s1, "s3": s3, "s4": s4, "ta": ta, "t0": t0, "t1": t1, "t2": t2, "t3": t3i, "e": t3e}
 
     def tick(i, carry):
         for name, piece, lag in ORDER:

time: 156 us -> 152 us (0.974)
  Pallas kernels: 153 us -> 149 us
    pallas_call x1, Pallas kernels: 153 us -> 149 us  [local_fn(): pl.pallas_call(functools.partial(kernel, n_row, n_col, norm), out_shape=(...]
where the time goes in v6:
time: 152 us; the launch traced here: 151 us
  Pallas kernels  149 us (98%)
  local copies, waits for them, and re-layouts  2.14 us (1%)
    pallas_call x1, Pallas kernels, local_fn(): pl.pallas_call(functools.partial(kernel, n_row, n_col, norm), out_shape=(...  149 us

profile of v6, /device:TPU:0, one launch (start us, length us, event | category | flops | bytes accessed | tf_op | source)
XLA Modules:
  0.0 151.4 jit_solution(4053065398593276340)
XLA Ops:
  0.6 148.6 %shard_map.67 = (f32[4,16,2304]{2,1,0:T(8,128)S(1)}, f32[4,16,2304]{2,1,0:T(8,128)S(1)}, f32[1,64]{1,0:T(1,128)S(1)}) custom-call(bf16[2304,2304]{1,0:T(8,128)(2,1)} %k_hbm.1, bf16[2304,2304]{1,0:T(8,128)(2,1)} %c_hbm.1, f32[4,16,2304]{2,1,0:T(8,128)} %bitcast.16, f32[4,16,2304]{2,1,0:T(8,128)} %bitcast.17), custom_call_target="tpu_custom_call" | custom-call | tf_op jit(solution)/shard_map/pallas_call | solution.py:340
  149.3 0.8 copy.10
  150.1 0.8 copy.11
  150.9 0.5 copy.12

commit v7 on v6

--- a/solution.py
+++ b/solution.py
@@ -19,10 +19,11 @@
 K_PIECES = (768, 768, 512, 256)
 KC_FIRST = 5
 ORDER = (
-    ("e", 1, 4), ("e", 2, 4), ("sa", 0, 0), ("ca", None, 0), ("e", 3, 4), ("t3", 0, 3), ("s4", 0, 1),
-    ("e", 4, 4), ("s1", None, 0), ("cost", None, 0), ("t3", 1, 3), ("s4", 1, 1), ("ta", 0, 1), ("s3", 0, 0),
-    ("t2", 0, 2), ("s3", 1, 0), ("t3", 2, 3), ("t2", 1, 2), ("t0", None, 1), ("t1", None, 1), ("t3", 3, 3),
-    ("t2", 2, 2), ("t3", 4, 3), ("e", 0, 3), ("kc", None, 0), ("t2", 3, 2), ("t2", 4, 2), ("kt", None, 0),
+    ("t3", 0, 3), ("s4", 0, 1), ("s4", 1, 1), ("s3", 0, 0), ("t3", 1, 3), ("ta", 0, 1), ("t2", 0, 2),
+    ("t0", None, 1), ("t3", 2, 3), ("s3", 1, 0), ("t1", None, 1), ("t2", 1, 2), ("t3", 3, 3), ("kc", None, 0),
+    ("e", 0, 3), ("e", 1, 3), ("e", 2, 3), ("t3", 4, 3), ("t2", 2, 2), ("kt", None, 0), ("sa", 0, -1),
+    ("ca", None, -1), ("e", 3, 3), ("t2", 3, 2), ("e", 4, 3), ("s1", None, -1), ("cost", None, -1),
+    ("t2", 4, 2),
 )
 
 
@@ -151,14 +152,32 @@
     early_spans = spans([sum(T_PIECES[c] for c in group) for group in EARLY])
     early = sum(w for _, w in early_spans)
 
-    def sa(q, b, par, last):
+    def s_drain(b, par):
+        for j in range(len(s_pieces)):
+            d_copy(b, j).wait_send()
+            y_copy(par, b, j).wait_send()
+
+    def t_drain(b, par):
+        @pl.when(inner)
+        def _():
+            for c in range(len(t_pieces)):
+                x_copy(par, b, c).wait_send()
+
+        @pl.when(edge)
+        def _():
+            for c in range(len(t_pieces)):
+                e_copy(b, c).wait_send()
+
+    def sa(q, b, par, sweep):
+        if q == 0:
+            pl.when(sweep > 1)(lambda: s_drain(b, 1 - par))
         k0, kw = early_spans[q]
         for dst, h0 in ((DS, sib0), (SP, own0)):
             for o, w in tiles(half):
                 part = dot_nn(VB[b, :, k0:k0 + kw], KT[k0:k0 + kw, at(h0 + o, w)])
                 dst[b, :, o:o + w] = part if q == 0 else dst[b, :, o:o + w] + part
 
-    def s1(b, par, last):
+    def s1(b, par, sweep):
         for j, (o0, width) in enumerate(s_pieces):
             for o, w in tiles(width):
                 o += o0
@@ -173,7 +192,7 @@
             for c in range(len(t_pieces)):
                 v_copy(b, c).wait_send()
 
-    def s3(j, b, par, last):
+    def s3(j, b, par, sweep):
         o, w = s_pieces[j]
         d_copy(b, j).wait_recv()
         SP[b, :, o:o + w] = SP[b, :, o:o + w] + DR[b, :, o:o + w]
@@ -181,7 +200,7 @@
         if j == len(s_pieces) - 1:
             v_drain(b)
 
-    def s4(j, b, par, last):
+    def s4(j, b, par, sweep):
         o, w = s_pieces[j]
         y_copy(par, b, j).wait_recv()
         sl = at(own0 + o, w)
@@ -190,21 +209,21 @@
         u_copy(b, j).start()
         UF[b, :, sl] = u
         if j == len(s_pieces) - 1:
-            pl.when(last)(lambda: uf_copy(b).start())
-        d_copy(b, j).wait_send()
-        y_copy(par, b, j).wait_send()
-
-    def t0(b, par, last):
+            pl.when(sweep == SWEEPS - 1)(lambda: uf_copy(b).start())
+
+    def t0(b, par, sweep):
         for j in range(len(s_pieces)):
             u_copy(b, j).wait()
 
-    def ta(q, b, par, last):
+    def ta(q, b, par, sweep):
+        if q == 0:
+            pl.when(sweep > 0)(lambda: t_drain(b, 1 - par))
         o0, width = spans(TA_PIECES)[q]
         for o, w in tiles(width):
             o += o0
             TP[b, :, o:o + w] = dot_nn(UB[b, :, at(own0, half)], K[at(own0, half), o:o + w])
 
-    def t1(b, par, last):
+    def t1(b, par, sweep):
         def products(send):
             for c, (o0, width) in enumerate(t_pieces):
                 for o, w in tiles(width):
@@ -216,7 +235,7 @@
         pl.when(edge)(lambda: products(True))
         pl.when(inner)(lambda: products(False))
 
-    def t2(c, b, par, last):
+    def t2(c, b, par, sweep):
         o, w = t_pieces[c]
 
         @pl.when(inner)
@@ -225,7 +244,7 @@
             TP[b, :, o:o + w] = TP[b, :, o:o + w] + EI[b, :, o:o + w]
             x_copy(par, b, c).start()
 
-    def t3i(c, b, par, last):
+    def t3i(c, b, par, sweep):
         o, w = t_pieces[c]
 
         @pl.when(inner)
@@ -235,14 +254,12 @@
             VB[b, :, o:o + w] = v.astype(BF16)
             v_copy(b, c).start()
             VF[b, :, o:o + w] = v
-            pl.when(last)(lambda: vf_copy(b, c).start())
-            x_copy(par, b, c).wait_send()
-
-    def t3e(c, b, par, last):
+            pl.when(sweep == SWEEPS - 1)(lambda: vf_copy(b, c).start())
+
+    def t3e(c, b, par, sweep):
         @pl.when(edge)
         def _():
             v_copy(b, c).wait_recv()
-            e_copy(b, c).wait_send()
 
     def cost_early(b):
         for o, w in tiles(n):
@@ -250,6 +267,8 @@
 
     def cost_part(b):
         v_drain(b)
+        s_drain(b, (SWEEPS - 1) % 2)
+        t_drain(b, (SWEEPS - 1) % 2)
         uf_copy(b).wait()
         acc = jnp.zeros((m, 128), F32)
         for o, w in tiles(n):
@@ -303,7 +322,7 @@
                 @pl.when(jnp.logical_and(g >= (NB if name[0] == "s" or name == "t0" else 0), g < total_inst))
                 def _():
                     sweep = lax.div(g, NB)
-                    fn(lax.rem(g, NB), lax.rem(sweep, 2), sweep == SWEEPS - 1)
+                    fn(lax.rem(g, NB), lax.rem(sweep, 2), sweep)
         return carry
 
     lax.fori_loop(1, total_inst + NB, tick, 0)

time: 152 us -> 156 us (1.026)
  Pallas kernels: 149 us -> 153 us
    pallas_call x1, Pallas kernels: 149 us -> 153 us  [local_fn(): pl.pallas_call(functools.partial(kernel, n_row, n_col, norm), out_shape=(...]
where the time goes in v7:
time: 156 us
  Pallas kernels  153 us (98%)
  local copies, waits for them, and re-layouts  2.14 us (1%)
    pallas_call x1, Pallas kernels, local_fn(): pl.pallas_call(functools.partial(kernel, n_row, n_col, norm), out_shape=(...  153 us

profile of v7, /device:TPU:0, one launch (start us, length us, event | category | flops | bytes accessed | tf_op | source)
XLA Modules:
  0.0 156.1 jit_solution(3783361622564636130)
XLA Ops:
  0.6 153.3 %shard_map.67 = (f32[4,16,2304]{2,1,0:T(8,128)S(1)}, f32[4,16,2304]{2,1,0:T(8,128)S(1)}, f32[1,64]{1,0:T(1,128)S(1)}) custom-call(bf16[2304,2304]{1,0:T(8,128)(2,1)} %k_hbm.1, bf16[2304,2304]{1,0:T(8,128)(2,1)} %c_hbm.1, f32[4,16,2304]{2,1,0:T(8,128)} %bitcast.16, f32[4,16,2304]{2,1,0:T(8,128)} %bitcast.17), custom_call_target="tpu_custom_call" | custom-call | tf_op jit(solution)/shard_map/pallas_call | solution.py:359
  153.9 0.8 copy.10
  154.7 0.8 copy.11
  155.5 0.5 copy.12

commit v8 on v7

--- a/solution.py
+++ b/solution.py
@@ -19,11 +19,10 @@
 K_PIECES = (768, 768, 512, 256)
 KC_FIRST = 5
 ORDER = (
-    ("t3", 0, 3), ("s4", 0, 1), ("s4", 1, 1), ("s3", 0, 0), ("t3", 1, 3), ("ta", 0, 1), ("t2", 0, 2),
-    ("t0", None, 1), ("t3", 2, 3), ("s3", 1, 0), ("t1", None, 1), ("t2", 1, 2), ("t3", 3, 3), ("kc", None, 0),
-    ("e", 0, 3), ("e", 1, 3), ("e", 2, 3), ("t3", 4, 3), ("t2", 2, 2), ("kt", None, 0), ("sa", 0, -1),
-    ("ca", None, -1), ("e", 3, 3), ("t2", 3, 2), ("e", 4, 3), ("s1", None, -1), ("cost", None, -1),
-    ("t2", 4, 2),
+    ("e", 0, 4), ("t2", 3, 3), ("e", 1, 4), ("e", 2, 4), ("kt", None, 0), ("sa", 0, 0), ("ca", None, 0),
+    ("s4", 0, 1), ("e", 3, 4), ("t2", 4, 3), ("e", 4, 4), ("s1", None, 0), ("cost", None, 0), ("t3", 0, 3),
+    ("s4", 1, 1), ("ta", 0, 1), ("s3", 0, 0), ("t3", 1, 3), ("t2", 0, 2), ("s3", 1, 0), ("t0", None, 1),
+    ("t3", 2, 3), ("t1", None, 1), ("t2", 1, 2), ("t3", 3, 3), ("t2", 2, 2), ("t3", 4, 3), ("kc", None, 0),
 )
 
 

time: 156 us -> 153 us (0.981)
  Pallas kernels: 153 us -> 150 us
    pallas_call x1, Pallas kernels: 153 us -> 150 us  [local_fn(): pl.pallas_call(functools.partial(kernel, n_row, n_col, norm), out_shape=(...]
where the time goes in v8:
time: 153 us
  Pallas kernels  150 us (98%)
  local copies, waits for them, and re-layouts  2.14 us (1%)
    pallas_call x1, Pallas kernels, local_fn(): pl.pallas_call(functools.partial(kernel, n_row, n_col, norm), out_shape=(...  150 us

profile of v8, /device:TPU:0, one launch (start us, length us, event | category | flops | bytes accessed | tf_op | source)
XLA Modules:
  0.0 152.9 jit_solution(13991061952131474749)
XLA Ops:
  0.6 150.1 %shard_map.67 = (f32[4,16,2304]{2,1,0:T(8,128)S(1)}, f32[4,16,2304]{2,1,0:T(8,128)S(1)}, f32[1,64]{1,0:T(1,128)S(1)}) custom-call(bf16[2304,2304]{1,0:T(8,128)(2,1)} %k_hbm.1, bf16[2304,2304]{1,0:T(8,128)(2,1)} %c_hbm.1, f32[4,16,2304]{2,1,0:T(8,128)} %bitcast.16, f32[4,16,2304]{2,1,0:T(8,128)} %bitcast.17), custom_call_target="tpu_custom_call" | custom-call | tf_op jit(solution)/shard_map/pallas_call | solution.py:358
  150.7 0.8 copy.10
  151.6 0.8 copy.11
  152.4 0.5 copy.12

commit v9 on v8

--- a/solution.py
+++ b/solution.py
@@ -19,10 +19,10 @@
 K_PIECES = (768, 768, 512, 256)
 KC_FIRST = 5
 ORDER = (
-    ("e", 0, 4), ("t2", 3, 3), ("e", 1, 4), ("e", 2, 4), ("kt", None, 0), ("sa", 0, 0), ("ca", None, 0),
-    ("s4", 0, 1), ("e", 3, 4), ("t2", 4, 3), ("e", 4, 4), ("s1", None, 0), ("cost", None, 0), ("t3", 0, 3),
-    ("s4", 1, 1), ("ta", 0, 1), ("s3", 0, 0), ("t3", 1, 3), ("t2", 0, 2), ("s3", 1, 0), ("t0", None, 1),
-    ("t3", 2, 3), ("t1", None, 1), ("t2", 1, 2), ("t3", 3, 3), ("t2", 2, 2), ("t3", 4, 3), ("kc", None, 0),
+    ("e", 1, 4), ("e", 2, 4), ("sa", 0, 0), ("ca", None, 0), ("e", 3, 4), ("t3", 0, 3), ("s4", 0, 1),
+    ("e", 4, 4), ("s1", None, 0), ("cost", None, 0), ("t3", 1, 3), ("s4", 1, 1), ("ta", 0, 1), ("s3", 0, 0),
+    ("t2", 0, 2), ("s3", 1, 0), ("t3", 2, 3), ("t2", 1, 2), ("t0", None, 1), ("t1", None, 1), ("t3", 3, 3),
+    ("t2", 2, 2), ("t3", 4, 3), ("e", 0, 3), ("kc", None, 0), ("t2", 3, 2), ("t2", 4, 2), ("kt", None, 0),
 )
 
 
@@ -93,6 +93,16 @@
 
     ACC[...] = jnp.zeros_like(ACC)
 
+    def kt(t):
+        rows = at(t * (n // 3), n // 3)
+
+        def turn(q, carry):
+            cols = at(q * 256, 256)
+            KT[cols, rows] = jnp.transpose(K[rows, cols])
+            return carry
+
+        lax.fori_loop(0, n // 256, turn, 0)
+
     ones = jnp.ones((16, n), BF16)
     for cp, (o, w) in zip(k_loads, spans(K_PIECES)):
         cp.wait()
@@ -104,6 +114,7 @@
     b_load.start()
     c_load.start()
     a_load.wait()
+    kt(0)
     for cp in r_copies:
         cp.wait()
     s0 = RX[0] + RX[1]
@@ -251,21 +262,27 @@
             x_copy(par, b, c).wait_recv()
             v = B[b, :, o:o + w] / (TP[b, :, o:o + w] + XR[par, b, :, o:o + w])
             VB[b, :, o:o + w] = v.astype(BF16)
-            v_copy(b, c).start()
             VF[b, :, o:o + w] = v
             pl.when(sweep == SWEEPS - 1)(lambda: vf_copy(b, c).start())
+            pl.when(sweep < SWEEPS - 1)(lambda: v_copy(b, c).start())
 
     def t3e(c, b, par, sweep):
-        @pl.when(edge)
+        o, w = t_pieces[c]
+
+        @pl.when(jnp.logical_and(edge, sweep < SWEEPS - 1))
         def _():
             v_copy(b, c).wait_recv()
+
+        @pl.when(jnp.logical_and(edge, sweep == SWEEPS - 1))
+        def _():
+            vf_copy(b, c).wait_recv()
+            VB[b, :, o:o + w] = VF[b, :, o:o + w].astype(BF16)
 
     def cost_early(b):
         for o, w in tiles(n):
             WP[:, o:o + w] = dot_nn(VB[b, :, :early], KCT[:early, o:o + w])
 
     def cost_part(b):
-        v_drain(b)
         s_drain(b, (SWEEPS - 1) % 2)
         t_drain(b, (SWEEPS - 1) % 2)
         uf_copy(b).wait()
@@ -277,7 +294,6 @@
         ACC[pl.ds(pl.multiple_of(b * m, m), m), :] = acc
         for c in range(len(t_pieces)):
             pl.when(inner)(lambda c=c: vf_copy(b, c).wait_send())
-            pl.when(edge)(lambda c=c: vf_copy(b, c).wait_recv())
 
     def kc(t):
         rows = at(t * 128, 128)
@@ -285,16 +301,6 @@
         def turn(q, carry):
             cols = at(q * 256, 256)
             KCT[cols, rows] = KT[cols, rows] * jnp.transpose(C[rows, cols])
-            return carry
-
-        lax.fori_loop(0, n // 256, turn, 0)
-
-    def kt(t):
-        rows = at(t * (n // 3), n // 3)
-
-        def turn(q, carry):
-            cols = at(q * 256, 256)
-            KT[cols, rows] = jnp.transpose(K[rows, cols])
             return carry
 
         lax.fori_loop(0, n // 256, turn, 0)
@@ -310,7 +316,7 @@
                 g = i - lag
                 pl.when(jnp.logical_and(g >= total_inst, g < total_inst + NB))(lambda: cost_early(g - total_inst))
             elif name == "kt":
-                pl.when(i < 4)(lambda: kt(i - 1))
+                pl.when(i < 3)(lambda: kt(i))
             elif name == "kc":
                 pl.when(i == KC_FIRST)(lambda: c_load.wait())
                 pl.when(jnp.logical_and(i >= KC_FIRST, i < KC_FIRST + n // 128))(lambda: kc(i - KC_FIRST))

time: 153 us -> 151 us (0.987)
  Pallas kernels: 150 us -> 148 us
    pallas_call x1, Pallas kernels: 150 us -> 148 us  [local_fn(): pl.pallas_call(functools.partial(kernel, n_row, n_col, norm), out_shape=(...]
where the time goes in v9:
time: 151 us; the launch traced here: 150 us
  Pallas kernels  148 us (98%)
  local copies, waits for them, and re-layouts  2.14 us (1%)
    pallas_call x1, Pallas kernels, local_fn(): pl.pallas_call(functools.partial(kernel, n_row, n_col, norm), out_shape=(...  148 us

profile of v9, /device:TPU:0, one launch (start us, length us, event | category | flops | bytes accessed | tf_op | source)
XLA Modules:
  0.0 150.5 jit_solution(6328094755199463458)
XLA Ops:
  0.6 147.7 %shard_map.67 = (f32[4,16,2304]{2,1,0:T(8,128)S(1)}, f32[4,16,2304]{2,1,0:T(8,128)S(1)}, f32[1,64]{1,0:T(1,128)S(1)}) custom-call(bf16[2304,2304]{1,0:T(8,128)(2,1)} %k_hbm.1, bf16[2304,2304]{1,0:T(8,128)(2,1)} %c_hbm.1, f32[4,16,2304]{2,1,0:T(8,128)} %bitcast.16, f32[4,16,2304]{2,1,0:T(8,128)} %bitcast.17), custom_call_target="tpu_custom_call" | custom-call | tf_op jit(solution)/shard_map/pallas_call | solution.py:364
  148.3 0.8 copy.10
  149.1 0.8 copy.11
  149.9 0.5 copy.12

commit v10 on v9

--- a/solution.py
+++ b/solution.py
@@ -19,10 +19,10 @@
 K_PIECES = (768, 768, 512, 256)
 KC_FIRST = 5
 ORDER = (
-    ("e", 1, 4), ("e", 2, 4), ("sa", 0, 0), ("ca", None, 0), ("e", 3, 4), ("t3", 0, 3), ("s4", 0, 1),
-    ("e", 4, 4), ("s1", None, 0), ("cost", None, 0), ("t3", 1, 3), ("s4", 1, 1), ("ta", 0, 1), ("s3", 0, 0),
-    ("t2", 0, 2), ("s3", 1, 0), ("t3", 2, 3), ("t2", 1, 2), ("t0", None, 1), ("t1", None, 1), ("t3", 3, 3),
-    ("t2", 2, 2), ("t3", 4, 3), ("e", 0, 3), ("kc", None, 0), ("t2", 3, 2), ("t2", 4, 2), ("kt", None, 0),
+    ("s4", 0, 1), ("t2", 1, 2), ("t3", 3, 3), ("s4", 1, 1), ("t3", 4, 3), ("s3", 0, 0), ("t2", 2, 2),
+    ("ta", 0, 1), ("t2", 3, 2), ("s3", 1, 0), ("t0", None, 1), ("t1", None, 1), ("t2", 4, 2), ("e", 0, 3),
+    ("kc", None, 0), ("e", 1, 3), ("t3", 0, 2), ("e", 2, 3), ("kt", None, 0), ("sa", 0, -1), ("ca", None, -1),
+    ("t3", 1, 2), ("t3", 2, 2), ("e", 3, 3), ("t2", 0, 1), ("e", 4, 3), ("s1", None, -1), ("cost", None, -1),
 )
 
 

time: 151 us -> 153 us (1.013)
  Pallas kernels: 148 us -> 150 us
    pallas_call x1, Pallas kernels: 148 us -> 150 us  [local_fn(): pl.pallas_call(functools.partial(kernel, n_row, n_col, norm), out_shape=(...]
where the time goes in v10:
time: 153 us
  Pallas kernels  150 us (98%)
  local copies, waits for them, and re-layouts  2.14 us (1%)
    pallas_call x1, Pallas kernels, local_fn(): pl.pallas_call(functools.partial(kernel, n_row, n_col, norm), out_shape=(...  150 us

profile of v10, /device:TPU:0, one launch (start us, length us, event | category | flops | bytes accessed | tf_op | source)
XLA Modules:
  0.0 153.0 jit_solution(12463606855526535192)
XLA Ops:
  0.6 150.2 %shard_map.67 = (f32[4,16,2304]{2,1,0:T(8,128)S(1)}, f32[4,16,2304]{2,1,0:T(8,128)S(1)}, f32[1,64]{1,0:T(1,128)S(1)}) custom-call(bf16[2304,2304]{1,0:T(8,128)(2,1)} %k_hbm.1, bf16[2304,2304]{1,0:T(8,128)(2,1)} %c_hbm.1, f32[4,16,2304]{2,1,0:T(8,128)} %bitcast.16, f32[4,16,2304]{2,1,0:T(8,128)} %bitcast.17), custom_call_target="tpu_custom_call" | custom-call | tf_op jit(solution)/shard_map/pallas_call | solution.py:364
  150.8 0.8 copy.10
  151.7 0.8 copy.11
  152.5 0.5 copy.12

commit v11 on v10

--- a/solution.py
+++ b/solution.py
@@ -16,13 +16,13 @@
 EARLY = ((0, 1, 2),)
 TA_PIECES = (2304,)
 S_PIECES = (512, 640)
-K_PIECES = (768, 768, 512, 256)
+K_PIECES = (256, 512, 768, 512, 256)
 KC_FIRST = 5
 ORDER = (
-    ("s4", 0, 1), ("t2", 1, 2), ("t3", 3, 3), ("s4", 1, 1), ("t3", 4, 3), ("s3", 0, 0), ("t2", 2, 2),
-    ("ta", 0, 1), ("t2", 3, 2), ("s3", 1, 0), ("t0", None, 1), ("t1", None, 1), ("t2", 4, 2), ("e", 0, 3),
-    ("kc", None, 0), ("e", 1, 3), ("t3", 0, 2), ("e", 2, 3), ("kt", None, 0), ("sa", 0, -1), ("ca", None, -1),
-    ("t3", 1, 2), ("t3", 2, 2), ("e", 3, 3), ("t2", 0, 1), ("e", 4, 3), ("s1", None, -1), ("cost", None, -1),
+    ("e", 2, 4), ("sa", 0, 0), ("ca", None, 0), ("t3", 0, 3), ("s4", 0, 1), ("e", 3, 4), ("e", 4, 4),
+    ("s1", None, 0), ("cost", None, 0), ("t3", 1, 3), ("s4", 1, 1), ("t2", 0, 2), ("t3", 2, 3), ("s3", 0, 0),
+    ("ta", 0, 1), ("t2", 1, 2), ("t3", 3, 3), ("s3", 1, 0), ("t3", 4, 3), ("t0", None, 1), ("t2", 2, 2),
+    ("t1", None, 1), ("t2", 3, 2), ("e", 0, 3), ("kc", None, 0), ("t2", 4, 2), ("e", 1, 3), ("kt", None, 0),
 )
 
 

time: 153 us -> 153 us (level)
  no operation moved by 1% of the time
where the time goes in v11:
time: 153 us
  Pallas kernels  150 us (98%)
  local copies, waits for them, and re-layouts  2.14 us (1%)
    pallas_call x1, Pallas kernels, local_fn(): pl.pallas_call(functools.partial(kernel, n_row, n_col, norm), out_shape=(...  150 us

profile of v11, /device:TPU:0, one launch (start us, length us, event | category | flops | bytes accessed | tf_op | source)
XLA Modules:
  0.0 153.2 jit_solution(3354850707308581159)
XLA Ops:
  0.6 150.4 %shard_map.67 = (f32[4,16,2304]{2,1,0:T(8,128)S(1)}, f32[4,16,2304]{2,1,0:T(8,128)S(1)}, f32[1,64]{1,0:T(1,128)S(1)}) custom-call(bf16[2304,2304]{1,0:T(8,128)(2,1)} %k_hbm.1, bf16[2304,2304]{1,0:T(8,128)(2,1)} %c_hbm.1, f32[4,16,2304]{2,1,0:T(8,128)} %bitcast.16, f32[4,16,2304]{2,1,0:T(8,128)} %bitcast.17), custom_call_target="tpu_custom_call" | custom-call | tf_op jit(solution)/shard_map/pallas_call | solution.py:364
  151.0 0.8 copy.10
  151.9 0.8 copy.11
  152.7 0.5 copy.12

commit v12 on v9

--- a/solution.py
+++ b/solution.py
@@ -69,6 +69,20 @@
     t_pieces = spans(T_PIECES)
     s_pieces = spans(S_PIECES)
 
+    mode = {"chip": None, "full": False}
+
+    def on_inner(fn):
+        if mode["chip"] is None:
+            pl.when(inner)(fn)
+        elif mode["chip"] == "inner":
+            fn()
+
+    def on_edge(fn):
+        if mode["chip"] is None:
+            pl.when(edge)(fn)
+        elif mode["chip"] == "edge":
+            fn()
+
     def at(o, w):
         return pl.ds(pl.multiple_of(o, 128), w)
 
@@ -168,12 +182,12 @@
             y_copy(par, b, j).wait_send()
 
     def t_drain(b, par):
-        @pl.when(inner)
+        @on_inner
         def _():
             for c in range(len(t_pieces)):
                 x_copy(par, b, c).wait_send()
 
-        @pl.when(edge)
+        @on_edge
         def _():
             for c in range(len(t_pieces)):
                 e_copy(b, c).wait_send()
@@ -197,7 +211,7 @@
             SP[b, :, o:o + w] += dot_nn(VB[b, :, early:], KT[early:, at(own0 + o, w)])
 
     def v_drain(b):
-        @pl.when(inner)
+        @on_inner
         def _():
             for c in range(len(t_pieces)):
                 v_copy(b, c).wait_send()
@@ -242,13 +256,13 @@
                 if send:
                     e_copy(b, c).start()
 
-        pl.when(edge)(lambda: products(True))
-        pl.when(inner)(lambda: products(False))
+        on_edge(lambda: products(True))
+        on_inner(lambda: products(False))
 
     def t2(c, b, par, sweep):
         o, w = t_pieces[c]
 
-        @pl.when(inner)
+        @on_inner
         def _():
             e_copy(b, c).wait_recv()
             TP[b, :, o:o + w] = TP[b, :, o:o + w] + EI[b, :, o:o + w]
@@ -257,26 +271,32 @@
     def t3i(c, b, par, sweep):
         o, w = t_pieces[c]
 
-        @pl.when(inner)
+        @on_inner
         def _():
             x_copy(par, b, c).wait_recv()
             v = B[b, :, o:o + w] / (TP[b, :, o:o + w] + XR[par, b, :, o:o + w])
             VB[b, :, o:o + w] = v.astype(BF16)
-            VF[b, :, o:o + w] = v
-            pl.when(sweep == SWEEPS - 1)(lambda: vf_copy(b, c).start())
-            pl.when(sweep < SWEEPS - 1)(lambda: v_copy(b, c).start())
+            if mode["full"]:
+                v_copy(b, c).start()
+            else:
+                VF[b, :, o:o + w] = v
+                pl.when(sweep == SWEEPS - 1)(lambda: vf_copy(b, c).start())
+                pl.when(sweep < SWEEPS - 1)(lambda: v_copy(b, c).start())
 
     def t3e(c, b, par, sweep):
         o, w = t_pieces[c]
 
-        @pl.when(jnp.logical_and(edge, sweep < SWEEPS - 1))
-        def _():
-            v_copy(b, c).wait_recv()
-
-        @pl.when(jnp.logical_and(edge, sweep == SWEEPS - 1))
-        def _():
+        def last():
             vf_copy(b, c).wait_recv()
             VB[b, :, o:o + w] = VF[b, :, o:o + w].astype(BF16)
+
+        @on_edge
+        def _():
+            if mode["full"]:
+                v_copy(b, c).wait_recv()
+            else:
+                pl.when(sweep < SWEEPS - 1)(lambda: v_copy(b, c).wait_recv())
+                pl.when(sweep == SWEEPS - 1)(last)
 
     def cost_early(b):
         for o, w in tiles(n):
@@ -293,7 +313,7 @@
                 acc = acc + p[:, q:q + 128]
         ACC[pl.ds(pl.multiple_of(b * m, m), m), :] = acc
         for c in range(len(t_pieces)):
-            pl.when(inner)(lambda c=c: vf_copy(b, c).wait_send())
+            on_inner(lambda c=c: vf_copy(b, c).wait_send())
 
     def kc(t):
         rows = at(t * 128, 128)
@@ -307,30 +327,45 @@
 
     steps = {"sa": sa, "s1": s1, "s3": s3, "s4": s4, "ta": ta, "t0": t0, "t1": t1, "t2": t2, "t3": t3i, "e": t3e}
 
+    def call(name, piece, g):
+        fn = steps[name] if piece is None else functools.partial(steps[name], piece)
+        sweep = lax.div(g, NB)
+        fn(lax.rem(g, NB), lax.rem(sweep, 2), sweep)
+
     def tick(i, carry):
         for name, piece, lag in ORDER:
-            if name == "cost":
-                g = i - lag
-                pl.when(jnp.logical_and(g >= total_inst, g < total_inst + NB))(lambda: cost_part(g - total_inst))
-            elif name == "ca":
-                g = i - lag
-                pl.when(jnp.logical_and(g >= total_inst, g < total_inst + NB))(lambda: cost_early(g - total_inst))
+            g = i - lag
+            if name in ("cost", "ca"):
+                fn = cost_part if name == "cost" else cost_early
+                pl.when(jnp.logical_and(g >= total_inst, g < total_inst + NB))(lambda: fn(g - total_inst))
             elif name == "kt":
                 pl.when(i < 3)(lambda: kt(i))
-            elif name == "kc":
-                pl.when(i == KC_FIRST)(lambda: c_load.wait())
-                pl.when(jnp.logical_and(i >= KC_FIRST, i < KC_FIRST + n // 128))(lambda: kc(i - KC_FIRST))
-            else:
-                g = i - lag
-                fn = steps[name] if piece is None else functools.partial(steps[name], piece)
-
-                @pl.when(jnp.logical_and(g >= (NB if name[0] == "s" or name == "t0" else 0), g < total_inst))
-                def _():
-                    sweep = lax.div(g, NB)
-                    fn(lax.rem(g, NB), lax.rem(sweep, 2), sweep)
+            elif name != "kc":
+                first = NB if name[0] == "s" or name == "t0" else 0
+                pl.when(jnp.logical_and(g >= first, g < total_inst))(lambda: call(name, piece, g))
         return carry
 
-    lax.fori_loop(1, total_inst + NB, tick, 0)
+    def full_tick(i):
+        for name, piece, lag in ORDER:
+            if name == "kc":
+                kc(i - KC_FIRST)
+            elif name not in ("cost", "ca", "kt"):
+                call(name, piece, i - lag)
+
+    full_end = KC_FIRST + n // 128
+    lax.fori_loop(1, KC_FIRST, tick, 0)
+    c_load.wait()
+    for chip, cond in (("inner", inner), ("edge", edge)):
+        @pl.when(cond)
+        def _(chip=chip):
+            def body(i, carry):
+                mode.update(chip=chip, full=True)
+                full_tick(i)
+                mode.update(chip=None, full=False)
+                return carry
+
+            lax.fori_loop(KC_FIRST, full_end, body, 0)
+    lax.fori_loop(full_end, total_inst + NB, tick, 0)
 
     tot = jnp.sum(jnp.transpose(ACC[...]), axis=0, keepdims=True)
     CPS[...] = jnp.broadcast_to(tot, CPS.shape)

time: 151 us -> 149 us (0.987)
  Pallas kernels: 148 us -> 146 us
where the time goes in v12:
time: 149 us
  Pallas kernels  146 us (98%)
  local copies, waits for them, and re-layouts  2.14 us (1%)
    pallas_call x1, Pallas kernels, local_fn(): pl.pallas_call(functools.partial(kernel, n_row, n_col, norm), out_shape=(...  146 us

profile of v12, /device:TPU:0, one launch (start us, length us, event | category | flops | bytes accessed | tf_op | source)
XLA Modules:
  0.0 149.2 jit_solution(3512945120108321399)
XLA Ops:
  0.6 146.4 %shard_map.67 = (f32[4,16,2304]{2,1,0:T(8,128)S(1)}, f32[4,16,2304]{2,1,0:T(8,128)S(1)}, f32[1,64]{1,0:T(1,128)S(1)}) custom-call(bf16[2304,2304]{1,0:T(8,128)(2,1)} %k_hbm.1, bf16[2304,2304]{1,0:T(8,128)(2,1)} %c_hbm.1, f32[4,16,2304]{2,1,0:T(8,128)} %bitcast.16, f32[4,16,2304]{2,1,0:T(8,128)} %bitcast.17), custom_call_target="tpu_custom_call" | custom-call | tf_op jit(solution)/shard_map/pallas_call | solution.py:399
  147.0 0.8 copy.10
  147.9 0.8 copy.11
  148.7 0.5 copy.12

commit v13 on v12

--- a/solution.py
+++ b/solution.py
@@ -16,7 +16,7 @@
 EARLY = ((0, 1, 2),)
 TA_PIECES = (2304,)
 S_PIECES = (512, 640)
-K_PIECES = (768, 768, 512, 256)
+K_PIECES = (256, 512, 768, 512, 256)
 KC_FIRST = 5
 ORDER = (
     ("e", 1, 4), ("e", 2, 4), ("sa", 0, 0), ("ca", None, 0), ("e", 3, 4), ("t3", 0, 3), ("s4", 0, 1),
@@ -131,11 +131,14 @@
     kt(0)
     for cp in r_copies:
         cp.wait()
-    s0 = RX[0] + RX[1]
-    for d in range(2, n_col):
-        s0 = s0 + RX[d]
-    for b in range(NB):
+
+    def first_u(b):
+        s0 = RX[0] + RX[1]
+        for d in range(2, n_col):
+            s0 = s0 + RX[d]
         UB[b] = (A[b] / s0).astype(BF16)
+
+    first_u(0)
     b_load.wait()
 
     def u_copy(b, j):
@@ -339,6 +342,7 @@
                 fn = cost_part if name == "cost" else cost_early
                 pl.when(jnp.logical_and(g >= total_inst, g < total_inst + NB))(lambda: fn(g - total_inst))
             elif name == "kt":
+                pl.when(i < NB)(lambda: first_u(i))
                 pl.when(i < 3)(lambda: kt(i))
             elif name != "kc":
                 first = NB if name[0] == "s" or name == "t0" else 0

time: 149 us -> 149 us (level)
  no operation moved by 1% of the time
where the time goes in v13:
time: 149 us
  Pallas kernels  146 us (98%)
  local copies, waits for them, and re-layouts  2.14 us (1%)
    pallas_call x1, Pallas kernels, local_fn(): pl.pallas_call(functools.partial(kernel, n_row, n_col, norm), out_shape=(...  146 us

profile of v13, /device:TPU:0, one launch (start us, length us, event | category | flops | bytes accessed | tf_op | source)
XLA Modules:
  0.0 149.2 jit_solution(9942396245075759636)
XLA Ops:
  0.6 146.4 %shard_map.67 = (f32[4,16,2304]{2,1,0:T(8,128)S(1)}, f32[4,16,2304]{2,1,0:T(8,128)S(1)}, f32[1,64]{1,0:T(1,128)S(1)}) custom-call(bf16[2304,2304]{1,0:T(8,128)(2,1)} %k_hbm.1, bf16[2304,2304]{1,0:T(8,128)(2,1)} %c_hbm.1, f32[4,16,2304]{2,1,0:T(8,128)} %bitcast.16, f32[4,16,2304]{2,1,0:T(8,128)} %bitcast.17), custom_call_target="tpu_custom_call" | custom-call | tf_op jit(solution)/shard_map/pallas_call | solution.py:403
  147.0 0.8 copy.10
  147.9 0.8 copy.11
  148.7 0.5 copy.12

commit v14 on v13

--- a/solution.py
+++ b/solution.py
@@ -19,10 +19,11 @@
 K_PIECES = (256, 512, 768, 512, 256)
 KC_FIRST = 5
 ORDER = (
-    ("e", 1, 4), ("e", 2, 4), ("sa", 0, 0), ("ca", None, 0), ("e", 3, 4), ("t3", 0, 3), ("s4", 0, 1),
-    ("e", 4, 4), ("s1", None, 0), ("cost", None, 0), ("t3", 1, 3), ("s4", 1, 1), ("ta", 0, 1), ("s3", 0, 0),
+    ("e", 1, 4), ("e", 2, 4), ("sa", 0, 0), ("e", 3, 4), ("t3", 0, 3), ("s4", 0, 1),
+    ("e", 4, 4), ("s1", None, 0), ("t3", 1, 3), ("s4", 1, 1), ("ta", 0, 1), ("s3", 0, 0),
     ("t2", 0, 2), ("s3", 1, 0), ("t3", 2, 3), ("t2", 1, 2), ("t0", None, 1), ("t1", None, 1), ("t3", 3, 3),
-    ("t2", 2, 2), ("t3", 4, 3), ("e", 0, 3), ("kc", None, 0), ("t2", 3, 2), ("t2", 4, 2), ("kt", None, 0),
+    ("t2", 2, 2), ("t3", 4, 3), ("e", 0, 3), ("kc", None, 0), ("t2", 3, 2), ("t2", 4, 2), ("ca", None, 0), ("cost", None, 0),
+    ("kt", None, 0),
 )
 
 

time: 149 us -> 150 us (level)
  no operation moved by 1% of the time
where the time goes in v14:
time: 150 us
  Pallas kernels  147 us (98%)
  local copies, waits for them, and re-layouts  2.14 us (1%)
    pallas_call x1, Pallas kernels, local_fn(): pl.pallas_call(functools.partial(kernel, n_row, n_col, norm), out_shape=(...  147 us

profile of v14, /device:TPU:0, one launch (start us, length us, event | category | flops | bytes accessed | tf_op | source)
XLA Modules:
  0.0 150.2 jit_solution(2859711233203920891)
XLA Ops:
  0.6 147.4 %shard_map.67 = (f32[4,16,2304]{2,1,0:T(8,128)S(1)}, f32[4,16,2304]{2,1,0:T(8,128)S(1)}, f32[1,64]{1,0:T(1,128)S(1)}) custom-call(bf16[2304,2304]{1,0:T(8,128)(2,1)} %k_hbm.1, bf16[2304,2304]{1,0:T(8,128)(2,1)} %c_hbm.1, f32[4,16,2304]{2,1,0:T(8,128)} %bitcast.16, f32[4,16,2304]{2,1,0:T(8,128)} %bitcast.17), custom_call_target="tpu_custom_call" | custom-call | tf_op jit(solution)/shard_map/pallas_call | solution.py:404
  148.0 0.8 copy.10
  148.8 0.8 copy.11
  149.6 0.5 copy.12
